TPU v7x, 128 devices: a whole 4x4x4 slice. The times are simulated.
128 devices in a mesh: outer: 8 (over z_hi, y), inner: 16 (over z_lo, x, core).
Axes of the slice: x: 4, y: 4, z: 4 (z_hi: 2, z_lo: 2; z = z_hi * 2 + z_lo), core: 2. Of those that a mesh axis runs over, the one named last changes fastest.
Arguments:
- query_rows: bfloat16 [16384, 4096], P(('outer', 'inner')), may hold values from -6 to 6
- key_rows: bfloat16 [16384, 4096], P(('outer', 'inner')), may hold values from -6 to 6
- value_rows: bfloat16 [16384, 4096], P(('outer', 'inner')), may hold values from -6 to 6
- out_grad: bfloat16 [16384, 4096], P(('outer', 'inner')), may hold values from -6 to 6
- filter_rows: bfloat16 [16384, 4096], P(('outer', 'inner')), may hold values from -0.046875 to 0.046875
- skip_gain: float32 [4096], replicated, may hold values from -1 to 1
Outputs:
- layer_out: bfloat16 [16384, 4096], P(('outer', 'inner'))
- query_grad: bfloat16 [16384, 4096], P(('outer', 'inner'))
- key_grad: bfloat16 [16384, 4096], P(('outer', 'inner'))
- value_grad: bfloat16 [16384, 4096], P(('outer', 'inner'))
- filter_grad: bfloat16 [16384, 4096], P(('outer', 'inner'))
- skip_grad: float32 [4096], replicated
All inputs are finite; a program needn't handle non-finite values.
Results may differ from a plain program's by a relative error of at most 0.0085.
Values may be sent and summed in bfloat16 or wider, within the bound.
A program may use at most 128 MiB of HBM per device.

v0:
```python
import math

import jax
import jax.numpy as jnp
from jax import lax
from jax.sharding import PartitionSpec as P

TWO_PI = 2.0 * math.pi


def in_blocks(value, dim, count):
    dims = value.shape
    tiles = value.reshape(*dims[:dim], count, dims[dim] // count, *dims[dim + 1 :])
    return jnp.moveaxis(tiles, dim, 0)


def cut_rows(length, count):
    turn = length // count
    if turn >= 8:
        turn -= turn % 8
    return [turn * k for k in range(1, count)]


def joined_along(tiles, dim):
    dims = list(tiles.shape[1:])
    dims[dim] *= tiles.shape[0]
    return jnp.moveaxis(tiles, 0, dim).reshape(dims)


def cut_exchange(value, axis, pieces, split_dim, concat_dim):
    tiles = in_blocks(value, split_dim, lax.axis_size(axis))
    cut = max(range(1, max(2, tiles.ndim - 1)), key=lambda d: tiles.shape[d])
    gathered = []
    for slab in jnp.split(tiles, cut_rows(tiles.shape[cut], pieces), axis=cut):
        if slab.size:
            gathered.append(lax.all_to_all(slab, axis, split_axis=0, concat_axis=0, tiled=True))
    return joined_along(jnp.concatenate(gathered, axis=cut), concat_dim)


def rounded_trig(phase, modulus):
    angle = (phase % modulus).astype(jnp.float32) * (TWO_PI / modulus)
    return (jnp.cos(angle).astype(jnp.bfloat16), jnp.sin(angle).astype(jnp.bfloat16))


def regroup_blocks(blocks):
    return cut_exchange(blocks, ("outer", "inner"), 2, 0, 0)


def body(query_rows, key_rows, value_rows, out_grad, filter_rows, skip_gain):
    devices = lax.axis_size(("outer", "inner"))
    position = lax.axis_index(("outer", "inner"))
    tokens_here = query_rows.shape[0]
    channels = query_rows.shape[1]
    piece_rows = tokens_here // devices
    length = tokens_here * devices
    points = 2 * length
    radix_count = 2 * devices
    factor = 1.0 / math.sqrt(length)
    product = (key_rows.astype(jnp.float32) * value_rows.astype(jnp.float32)).astype(jnp.bfloat16)
    gate_grad = out_grad.astype(jnp.float32) * query_rows.astype(jnp.float32)
    signals = jnp.stack([product, gate_grad.astype(jnp.bfloat16), filter_rows], axis=1)
    columns = regroup_blocks(signals.reshape(devices, piece_rows, 3, channels))
    anchor = jnp.arange(devices, dtype=jnp.int32)
    halves = jnp.arange(2, dtype=jnp.int32)
    local_steps = jnp.arange(piece_rows, dtype=jnp.int32)
    step_index = jnp.arange(tokens_here, dtype=jnp.int32)
    sample = position * piece_rows + local_steps
    section_one = []
    for half in range(2):
        freq_one = half * devices + anchor
        phase = (
            anchor[None, None, :] * freq_one[None, :, None] * tokens_here
            + sample[:, None, None] * freq_one[None, :, None]
        )
        one_cos, one_sin = rounded_trig(phase, points)
        table_one = jnp.stack([one_cos, -one_sin], axis=2).reshape(piece_rows, 2 * devices, devices)
        result = jnp.einsum(
            "skr,rsbc->ksbc", table_one, columns, preferred_element_type=jnp.float32
        )
        section_one.append(result.astype(jnp.bfloat16).reshape(devices, 2, piece_rows, 3, channels))
    section_one = regroup_blocks(jnp.stack(section_one, axis=2))
    full_sample = anchor[:, None] * piece_rows + local_steps[None, :]
    step_cos, step_sin = rounded_trig(
        full_sample[:, :, None] * step_index[None, None, :], tokens_here
    )
    real_col = jnp.stack([step_cos, step_sin])
    imag_col = jnp.stack([-step_sin, step_cos])
    table_two = jnp.stack([real_col, imag_col], axis=3)
    section_three = []
    for half in range(2):
        spectra = jnp.einsum(
            "oisbc,iosjk->jkbc",
            section_one[:, :, half],
            table_two,
            preferred_element_type=jnp.float32,
        )
        spec_real, spec_imag = (spectra[0], spectra[1])
        value_real, gate_real, filter_real = (spec_real[:, 0], spec_real[:, 1], spec_real[:, 2])
        value_imag, gate_imag, filter_imag = (spec_imag[:, 0], spec_imag[:, 1], spec_imag[:, 2])
        forward_real = value_real * filter_real - value_imag * filter_imag
        forward_imag = value_real * filter_imag + value_imag * filter_real
        backward_real = filter_real * gate_real + filter_imag * gate_imag
        backward_imag = filter_real * gate_imag - filter_imag * gate_real
        lag_real = (value_real * gate_real + value_imag * gate_imag) * factor
        lag_imag = (value_real * gate_imag - value_imag * gate_real) * factor
        products = jnp.stack(
            [
                jnp.stack([forward_real, backward_real, lag_real], axis=1),
                jnp.stack([forward_imag, backward_imag, lag_imag], axis=1),
            ]
        ).astype(jnp.bfloat16)
        freq_held = half * devices + position
        phase_three = (
            step_index[None, :] * step_index[:, None] * radix_count
            + step_index[None, :] * freq_held
        )
        three_cos, three_sin = rounded_trig(phase_three, points)
        real_row = jnp.stack([three_cos, -three_sin])
        imag_row = jnp.stack([three_sin, three_cos])
        table_three = jnp.stack([real_row, imag_row], axis=2)
        result = jnp.einsum(
            "ikbc,ikjs->sjbc", products, table_three, preferred_element_type=jnp.float32
        )
        section_three.append(result.astype(jnp.bfloat16))
    section_three = jnp.stack(section_three, axis=2).reshape(devices, piece_rows, 2, 2, 3, channels)
    rows_back = regroup_blocks(section_three)
    freq_last = halves[:, None] * devices + anchor[None, :]
    last_cos, last_sin = rounded_trig(anchor[None, None, :] * freq_last[:, :, None], radix_count)
    table_four = jnp.stack([last_cos, -last_sin])
    restored = (
        jnp.einsum("opjhbc,jhor->rpbc", rows_back, table_four, preferred_element_type=jnp.float32)
        / points
    )
    home_rows = regroup_blocks(restored.astype(jnp.bfloat16)).reshape(tokens_here, 3, channels)
    convolved = home_rows[:, 0].astype(jnp.float32)
    correlated = home_rows[:, 1].astype(jnp.float32)
    filter_grad = home_rows[:, 2]
    product_full = product.astype(jnp.float32)
    mixing = convolved + skip_gain[None, :] * product_full
    layer_out = (query_rows.astype(jnp.float32) * mixing).astype(jnp.bfloat16)
    query_grad = (out_grad.astype(jnp.float32) * mixing).astype(jnp.bfloat16)
    carried = correlated + skip_gain[None, :] * gate_grad
    key_grad = (carried * value_rows.astype(jnp.float32)).astype(jnp.bfloat16)
    value_grad = (carried * key_rows.astype(jnp.float32)).astype(jnp.bfloat16)
    skip_part = jnp.sum(gate_grad * product_full, axis=0)
    skip_sum = lax.psum(skip_part, ("outer", "inner"))
    return (layer_out, query_grad, key_grad, value_grad, filter_grad, skip_sum * factor)


def solution(mesh):
    return jax.shard_map(
        body,
        mesh=mesh,
        in_specs=(
            P(("outer", "inner"), None),
            P(("outer", "inner"), None),
            P(("outer", "inner"), None),
            P(("outer", "inner"), None),
            P(("outer", "inner"), None),
            P(),
        ),
        out_specs=(
            P(("outer", "inner"), None),
            P(("outer", "inner"), None),
            P(("outer", "inner"), None),
            P(("outer", "inner"), None),
            P(("outer", "inner"), None),
            P(),
        ),
        check_vma=False,
    )
```

profile of v0, /device:TPU:1, one launch (start us, length us, event | category | flops | bytes accessed | tf_op | source)
XLA Modules:
  0.0 723.8 jit_solution(18263861373759580703)
XLA Ops:
  12.8 11.9 %all-to-all-start = ((bf16[128,2,2048]{2,1,0:T(2,128)(2,1)}), bf16[128,2,2048]{2,1,0:T(2,128)(2,1)}, u32[]{:S(2)}, u32[]{:S(2)}) async-start(bf16[128,2,2048]{2,1,0:T(2,128)(2,1)} %reshape.865), calls=%async_computation | async-start | bytes 2097152 | tf_op jit(solution)/shard_map/all_to_all | solution.py:36
  28.4 15.6 %all-to-all-done = bf16[128,2,2048]{2,1,0:T(2,128)(2,1)} async-done(((bf16[128,2,2048]{2,1,0:T(2,128)(2,1)}), bf16[128,2,2048]{2,1,0:T(2,128)(2,1)}, u32[]{:S(2)}, u32[]{:S(2)}) %all-to-all-start) | async-done | bytes 1048608 | tf_op jit(solution)/shard_map/all_to_all | solution.py:36
  58.6 21.2 %all-to-all-done.1 = bf16[128,1,1,2,4096]{4,3,2,1,0:T(2,128)(2,1)} async-done(((bf16[128,1,1,2,4096]{4,3,2,1,0:T(2,128)(2,1)}), bf16[128,1,1,2,4096]{4,3,2,1,0:T(2,128)(2,1)}, u32[]{:S(2)}, u32[]{:S(2)}) %all-to-all-start.1) | async-done | bytes 2097184 | tf_op jit(solution)/shard_map/all_to_all | solution.py:36
  87.2 10.9 %stack_reshape.6 = bf16[128,2,1,1,3,4096]{5,1,0,4,3,2:T(2,128)(2,1)} reshape(bf16[256,1,3,4096]{3,0,2,1:T(8,128)(2,1)} %fusion.8) | data formatting | bytes 12582912 | tf_op jit(solution)/shard_map/stack;reshape | solution.py:81
  102.5 10.9 %stack_reshape.7 = bf16[128,2,1,1,3,4096]{5,1,0,4,3,2:T(2,128)(2,1)} reshape(bf16[256,1,3,4096]{3,0,2,1:T(8,128)(2,1)} %fusion.9) | data formatting | bytes 12582912 | tf_op jit(solution)/shard_map/stack;reshape | solution.py:81
  113.4 18.4 %copy_bitcast_fusion = bf16[128,1,2,2,1,3,4096]{6,2,5,3,4,1,0:T(2,128)(2,1)} fusion(bf16[128,2,1,1,3,4096]{5,1,0,4,3,2:T(2,128)(2,1)} %stack_reshape.7, bf16[128,2,1,1,3,4096]{5,1,0,4,3,2:T(2,128)(2,1)} %stack_reshape.6), kind=kLoop, calls=%fused_computation.9 | loop fusion | flops 6291456 | bytes 25165824 | tf_op jit(solution)/shard_map/reshape | solution.py:13
  131.8 12.0 %split.34 = bf16[128,1,2,2,1,1,4096]{6,2,5,3,4,1,0:T(2,128)(2,1)} slice(bf16[128,1,2,2,1,3,4096]{6,2,5,3,4,1,0:T(2,128)(2,1)} %copy_bitcast_fusion), slice={[0:128], [0:1], [0:2], [0:2], [0:1], [0:1], [0:4096]} | slice | bytes 8388608 | tf_op jit(solution)/shard_map/split | solution.py:34
  149.2 9.0 %split.35 = bf16[128,1,2,2,1,2,4096]{6,2,5,3,4,1,0:T(2,128)(2,1)} slice(bf16[128,1,2,2,1,3,4096]{6,2,5,3,4,1,0:T(2,128)(2,1)} %copy_bitcast_fusion), slice={[0:128], [0:1], [0:2], [0:2], [0:1], [1:3], [0:4096]} | slice | bytes 16777216 | tf_op jit(solution)/shard_map/split | solution.py:34
  158.2 43.4 %all-to-all-done.2 = bf16[128,1,2,2,1,1,4096]{6,2,5,3,4,1,0:T(2,128)(2,1)} async-done(((bf16[128,1,2,2,1,1,4096]{6,2,5,3,4,1,0:T(2,128)(2,1)}), bf16[128,1,2,2,1,1,4096]{6,2,5,3,4,1,0:T(2,128)(2,1)}, u32[]{:S(2)}, u32[]{:S(2)}) %all-to-all-start.2) | async-done | bytes 4194336 | tf_op jit(solution)/shard_map/all_to_all | solution.py:36
  210.6 7.1 copy.66
  217.7 93.1 %all-to-all-done.3 = bf16[128,1,2,2,1,2,4096]{6,2,5,3,4,1,0:T(2,128)(2,1)} async-done(((bf16[128,1,2,2,1,2,4096]{6,2,5,3,4,1,0:T(2,128)(2,1)}), bf16[128,1,2,2,1,2,4096]{6,2,5,3,4,1,0:T(2,128)(2,1)}, u32[]{:S(2)}, u32[]{:S(2)}) %all-to-all-start.3) | async-done | bytes 8388640 | tf_op jit(solution)/shard_map/all_to_all | solution.py:36
  310.8 12.9 %copy.67 = bf16[128,1,2,2,1,2,4096]{6,0,2,5,3,4,1:T(8,128)(2,1)} copy(bf16[128,1,2,2,1,2,4096]{6,2,5,3,4,1,0:T(2,128)(2,1)} %all-to-all-done.3) | data formatting | bytes 16777216 | tf_op jit(solution)/shard_map/all_to_all | solution.py:36
  340.4 8.5 %slice_bitcast_fusion.5 = (f32[128,3,4096]{2,0,1:T(8,128)S(1)}, f32[128,3,4096]{2,0,1:T(8,128)}) fusion(f32[2,128,3,4096]{3,1,2,0:T(8,128)} %convolution_bitcast_fusion.1), kind=kLoop, calls=%fused_computation.18 | loop fusion | bytes 25165824 | tf_op jit(solution)/shard_map/squeeze | solution.py:97
  365.2 8.4 %slice_bitcast_fusion.1 = (f32[128,3,4096]{2,0,1:T(8,128)S(1)}, f32[128,3,4096]{2,0,1:T(8,128)}) fusion(f32[2,128,3,4096]{3,1,2,0:T(8,128)} %convolution_bitcast_fusion), kind=kLoop, calls=%fused_computation.15 | loop fusion | bytes 25165824 | tf_op jit(solution)/shard_map/squeeze | solution.py:97
  400.0 10.7 %all-to-all-start.4 = ((bf16[128,1,1,2,2,1,4096]{6,4,5,3,2,1,0:T(2,128)(2,1)}), bf16[128,1,1,2,2,1,4096]{6,4,5,3,2,1,0:T(2,128)(2,1)}, u32[]{:S(2)}, u32[]{:S(2)}) async-start(bf16[128,1,1,2,2,1,4096]{6,4,5,3,2,1,0:T(2,128)(2,1)} %copy.70), calls=%async_computation.4 | async-start | bytes 8388608 | tf_op jit(solution)/shard_map/all_to_all | solution.py:36
  410.7 7.7 %split.37 = bf16[128,1,1,2,2,2,4096]{6,0,5,3,4,2,1:T(8,128)(2,1)} slice(bf16[128,1,1,2,2,3,4096]{6,0,5,3,4,2,1:T(8,128)(2,1)} %copy-done.2), slice={[0:128], [0:1], [0:1], [0:2], [0:2], [1:3], [0:4096]} | slice | bytes 16777216 | tf_op jit(solution)/shard_map/split | solution.py:34
  418.4 16.3 %copy.71 = bf16[128,1,1,2,2,2,4096]{6,5,3,4,2,1,0:T(2,128)(2,1)} copy(bf16[128,1,1,2,2,2,4096]{6,0,5,3,4,2,1:T(8,128)(2,1)} %split.37) | data formatting | bytes 16777216 | tf_op jit(solution)/shard_map/split | solution.py:34
  434.7 28.3 %all-to-all-done.4 = bf16[128,1,1,2,2,1,4096]{6,4,5,3,2,1,0:T(2,128)(2,1)} async-done(((bf16[128,1,1,2,2,1,4096]{6,4,5,3,2,1,0:T(2,128)(2,1)}), bf16[128,1,1,2,2,1,4096]{6,4,5,3,2,1,0:T(2,128)(2,1)}, u32[]{:S(2)}, u32[]{:S(2)}) %all-to-all-start.4) | async-done | bytes 4194336 | tf_op jit(solution)/shard_map/all_to_all | solution.py:36
  471.0 7.1 copy.72
  478.1 94.0 %all-to-all-done.5 = bf16[128,1,1,2,2,2,4096]{6,5,3,4,2,1,0:T(2,128)(2,1)} async-done(((bf16[128,1,1,2,2,2,4096]{6,5,3,4,2,1,0:T(2,128)(2,1)}), bf16[128,1,1,2,2,2,4096]{6,5,3,4,2,1,0:T(2,128)(2,1)}, u32[]{:S(2)}, u32[]{:S(2)}) %all-to-all-start.5) | async-done | bytes 8388640 | tf_op jit(solution)/shard_map/all_to_all | solution.py:36
  572.1 12.9 %copy.73 = bf16[128,1,1,2,2,2,4096]{6,0,3,5,4,2,1:T(8,128)(2,1)} copy(bf16[128,1,1,2,2,2,4096]{6,5,3,4,2,1,0:T(2,128)(2,1)} %all-to-all-done.5) | data formatting | bytes 16777216 | tf_op jit(solution)/shard_map/all_to_all | solution.py:36
  594.4 10.2 %all-to-all-start.6 = ((bf16[128,2,2048]{2,1,0:T(2,128)(2,1)}), bf16[128,2,2048]{2,1,0:T(2,128)(2,1)S(1)}, u32[]{:S(2)}, u32[]{:S(2)}) async-start(bf16[128,2,2048]{2,1,0:T(2,128)(2,1)} %reshape.867), calls=%async_computation.6 | async-start | bytes 2097152 | tf_op jit(solution)/shard_map/all_to_all | solution.py:36
  610.0 14.3 %all-to-all-done.6 = bf16[128,2,2048]{2,1,0:T(2,128)(2,1)S(1)} async-done(((bf16[128,2,2048]{2,1,0:T(2,128)(2,1)}), bf16[128,2,2048]{2,1,0:T(2,128)(2,1)S(1)}, u32[]{:S(2)}, u32[]{:S(2)}) %all-to-all-start.6) | async-done | bytes 1048608 | tf_op jit(solution)/shard_map/all_to_all | solution.py:36
  629.5 81.8 %psum.7 = f32[4096]{0:T(1024)S(1)} all-reduce(f32[4096]{0:T(1024)S(1)} %copy-done.20), channel_id=1, replica_groups=mesh['outer'=8,'inner'=16] {'outer','inner'}, use_global_device_ids=true, to_apply=%region_1.2 | all-reduce | flops 4096 | bytes 32768 | tf_op jit(solution)/shard_map/psum | solution.py:146
  (123 shorter events, 155.9 us)
Async XLA Ops:
  0.6 3.7 copy-start.19
  12.8 31.2 %all-to-all-start = ((bf16[128,2,2048]{2,1,0:T(2,128)(2,1)}), bf16[128,2,2048]{2,1,0:T(2,128)(2,1)}, u32[]{:S(2)}, u32[]{:S(2)}) async-start(bf16[128,2,2048]{2,1,0:T(2,128)(2,1)} %reshape.865), calls=%async_computation | async-start | bytes 2097152 | tf_op jit(solution)/shard_map/all_to_all | solution.py:36
  44.0 35.8 %all-to-all-start.1 = ((bf16[128,1,1,2,4096]{4,3,2,1,0:T(2,128)(2,1)}), bf16[128,1,1,2,4096]{4,3,2,1,0:T(2,128)(2,1)}, u32[]{:S(2)}, u32[]{:S(2)}) async-start(bf16[128,1,1,2,4096]{4,3,2,1,0:T(2,128)(2,1)} %copy.59), calls=%async_computation.1 | async-start | bytes 4194304 | tf_op jit(solution)/shard_map/all_to_all | solution.py:36
  143.8 57.8 %all-to-all-start.2 = ((bf16[128,1,2,2,1,1,4096]{6,2,5,3,4,1,0:T(2,128)(2,1)}), bf16[128,1,2,2,1,1,4096]{6,2,5,3,4,1,0:T(2,128)(2,1)}, u32[]{:S(2)}, u32[]{:S(2)}) async-start(bf16[128,1,2,2,1,1,4096]{6,2,5,3,4,1,0:T(2,128)(2,1)} %split.34), calls=%async_computation.2 | async-start | bytes 8388608 | tf_op jit(solution)/shard_map/all_to_all | solution.py:36
  201.6 109.2 %all-to-all-start.3 = ((bf16[128,1,2,2,1,2,4096]{6,2,5,3,4,1,0:T(2,128)(2,1)}), bf16[128,1,2,2,1,2,4096]{6,2,5,3,4,1,0:T(2,128)(2,1)}, u32[]{:S(2)}, u32[]{:S(2)}) async-start(bf16[128,1,2,2,1,2,4096]{6,2,5,3,4,1,0:T(2,128)(2,1)} %split.35), calls=%async_computation.3 | async-start | bytes 16777216 | tf_op jit(solution)/shard_map/all_to_all | solution.py:36
  310.8 12.9 %copy-start.4 = (bf16[128,1,2,2,1,1,4096]{6,0,2,5,3,4,1:T(8,128)(2,1)S(1)}, bf16[128,1,2,2,1,1,4096]{6,0,2,5,3,4,1:T(8,128)(2,1)}, u32[]{:S(2)}) copy-start(bf16[128,1,2,2,1,1,4096]{6,0,2,5,3,4,1:T(8,128)(2,1)} %copy.66) | copy-start | bytes 12582916
  330.4 4.5 copy-start.3
  348.9 5.6 copy-start
  348.9 8.5 %slice-start = ((s8[12582912]{0:T(1024)(128)(4,1)}), s8[4194304]{0:T(1024)(128)(4,1)S(1)}, s32[]{:S(2)}) async-start(s8[12582912]{0:T(1024)(128)(4,1)} %bitcast.169), calls=%async_computation.8 | async-start | bytes 8388608
  348.9 9.3 %slice-start.1 = ((s8[12582912]{0:T(1024)(128)(4,1)}), s8[4194304]{0:T(1024)(128)(4,1)S(1)}, s32[]{:S(2)}) async-start(s8[12582912]{0:T(1024)(128)(4,1)} %bitcast.169), calls=%async_computation.9 | async-start | bytes 8388608
  354.5 5.2 slice-start.2
  373.6 4.7 copy-start.1
  388.5 4.5 copy-start.2
  400.0 63.0 %all-to-all-start.4 = ((bf16[128,1,1,2,2,1,4096]{6,4,5,3,2,1,0:T(2,128)(2,1)}), bf16[128,1,1,2,2,1,4096]{6,4,5,3,2,1,0:T(2,128)(2,1)}, u32[]{:S(2)}, u32[]{:S(2)}) async-start(bf16[128,1,1,2,2,1,4096]{6,4,5,3,2,1,0:T(2,128)(2,1)} %copy.70), calls=%async_computation.4 | async-start | bytes 8388608 | tf_op jit(solution)/shard_map/all_to_all | solution.py:36
  463.0 109.2 %all-to-all-start.5 = ((bf16[128,1,1,2,2,2,4096]{6,5,3,4,2,1,0:T(2,128)(2,1)}), bf16[128,1,1,2,2,2,4096]{6,5,3,4,2,1,0:T(2,128)(2,1)}, u32[]{:S(2)}, u32[]{:S(2)}) async-start(bf16[128,1,1,2,2,2,4096]{6,5,3,4,2,1,0:T(2,128)(2,1)} %copy.71), calls=%async_computation.5 | async-start | bytes 16777216 | tf_op jit(solution)/shard_map/all_to_all | solution.py:36
  572.1 12.9 %copy-start.9 = (bf16[128,1,1,2,2,1,4096]{6,0,3,5,4,2,1:T(8,128)(2,1)S(1)}, bf16[128,1,1,2,2,1,4096]{6,0,3,5,4,2,1:T(8,128)(2,1)}, u32[]{:S(2)}) copy-start(bf16[128,1,1,2,2,1,4096]{6,0,3,5,4,2,1:T(8,128)(2,1)} %copy.72) | copy-start | bytes 12582916
  594.4 29.9 %all-to-all-start.6 = ((bf16[128,2,2048]{2,1,0:T(2,128)(2,1)}), bf16[128,2,2048]{2,1,0:T(2,128)(2,1)S(1)}, u32[]{:S(2)}, u32[]{:S(2)}) async-start(bf16[128,2,2048]{2,1,0:T(2,128)(2,1)} %reshape.867), calls=%async_computation.6 | async-start | bytes 2097152 | tf_op jit(solution)/shard_map/all_to_all | solution.py:36
  610.0 19.5 %copy-start.20 = (f32[4096]{0:T(1024)S(1)}, f32[4096]{0:T(1024)}, u32[]{:S(2)}) copy-start(f32[4096]{0:T(1024)} %get-tuple-element.6) | copy-start | bytes 49156
  624.3 89.7 %all-to-all-start.7 = ((bf16[128,1,1,2,4096]{4,3,2,1,0:T(2,128)(2,1)}), bf16[128,1,1,2,4096]{4,3,2,1,0:T(2,128)(2,1)}, u32[]{:S(2)}, u32[]{:S(2)}) async-start(bf16[128,1,1,2,4096]{4,3,2,1,0:T(2,128)(2,1)} %copy.75), calls=%async_computation.7 | async-start | bytes 4194304 | tf_op jit(solution)/shard_map/all_to_all | solution.py:36
  717.0 1.9 copy-start.14
  717.0 2.2 copy-start.15
  717.0 2.5 copy-start.16
  717.0 2.8 copy-start.17
  717.0 2.8 copy-start.21
  (9 other events, 13.4 us)
where the time goes:
time: 730 us; the launch traced here: 724 us
  waiting for transfers between devices  310 us (42%)
  local copies, waits for them, and re-layouts  180 us (25%)
  blocking collectives  81.8 us (11%)
  starting transfers between devices  62.8 us (9%)
  other arithmetic  59.3 us (8%)
  matrix products  29 us (4%)
    all_to_all x8, waiting for transfers between devices, cut_exchange(): lax.all_to_all(slab, axis, split_axis=0, concat_axis=0, tiled=True)  310 us
    psum x1, blocking collectives, body(): skip_sum = lax.psum(skip_part, ('outer', 'inner'))  81.8 us
    all_to_all x8, starting transfers between devices, cut_exchange(): lax.all_to_all(slab, axis, split_axis=0, concat_axis=0, tiled=True)  62.8 us
    split x13, local copies, waits for them, and re-layouts, cut_exchange(): jnp.split(tiles, cut_rows(tiles.shape[cut], pieces), axis=cut)  62.5 us
    all_to_all x8, local copies, waits for them, and re-layouts, cut_exchange(): lax.all_to_all(slab, axis, split_axis=0, concat_axis=0, tiled=True)  48.1 us
    unnamed x54, local copies, waits for them, and re-layouts  29.2 us
    another operation x2, local copies, waits for them, and re-layouts, body(): section_one = regroup_blocks(jnp.stack(section_one, axis=2))  21.8 us
    reshape x1, other arithmetic, in_blocks(): value.reshape(*dims[:dim], count, dims[dim] // count, *dims[dim + 1:])  18.4 us
  transfers between devices with their start and end apart: 8, of which 7 were waited for; matrix products, arithmetic and copies ran while one was open for 10% of the time, Pallas kernels for 0%

commit v1 on v0

v1 whole, which is shorter than its diff:
```python
import functools
import math

import jax
import jax.numpy as jnp
import numpy as np
from jax import lax
from jax.experimental import pallas as pl
from jax.experimental.pallas import tpu as pltpu
from jax.sharding import PartitionSpec as P

MESH = pl.DeviceIdType.MESH
BF = jnp.bfloat16
F32 = jnp.float32
DEVICES = 128
GROUPS = 4
ORDER = 91


def coefficient_tables(tokens, devices, length):
    pos = np.arange(devices, dtype=np.float64)
    freq = np.arange(devices, dtype=np.float64) + 0.5
    step = np.arange(tokens, dtype=np.float64)
    one = 2.0 * np.pi * np.outer(freq, pos) / (2 * devices)
    first = np.zeros((2, 2, devices, devices, 2))
    for e in range(2):
        first[e, 0, :, :, e] = np.cos(one)
        first[e, 1, :, :, e] = -np.sin(one)
    first = first.reshape(4 * devices, 2 * devices)
    last = np.transpose(first) * (2.0 / (2 * length))
    two = 2.0 * np.pi * (np.outer(step, step) % tokens) / tokens
    c, s = np.cos(two), np.sin(two)
    forth = np.block([[c, -s], [s, c]])
    back = np.block([[c, s], [-s, c]])
    turn = 2.0 * np.pi * np.outer(freq, step) / (2 * length)
    as_bf = lambda t: np.asarray(t, np.float32).astype(jnp.bfloat16)
    return (
        as_bf(first),
        as_bf(forth),
        as_bf(back),
        as_bf(last),
        np.stack([np.cos(turn), np.sin(turn)]).astype(np.float32),
    )


def kernel(
    q_hbm,
    k_hbm,
    v_hbm,
    g_hbm,
    h_hbm,
    gain_ref,
    t1_ref,
    t2_ref,
    t3_ref,
    t4_ref,
    tw_ref,
    lo_hbm,
    qg_hbm,
    kg_hbm,
    vg_hbm,
    fg_hbm,
    sk_ref,
    ins,
    outs,
    packed,
    held,
    made,
    back,
    part,
    spec,
    sk_own,
    sk_all,
    load_sem,
    store_sem,
    in_send,
    in_recv,
    out_send,
    out_recv,
    sk_send,
    sk_recv,
):
    tokens, channels = q_hbm.shape
    width = channels // GROUPS
    per = width // DEVICES
    pairs = per // 2
    outer = lax.axis_index("outer")
    inner = lax.axis_index("inner")
    me = outer * 16 + inner
    my_y, my_zh = lax.rem(outer, 4), lax.div(outer, 4)
    my_c, my_x, my_zl = lax.rem(inner, 2), lax.rem(lax.div(inner, 2), 4), lax.div(inner, 8)
    my_z = my_zh * 2 + my_zl

    def target(k):
        j = lax.rem(k * ORDER, DEVICES)
        c = lax.rem(my_c + j, 2)
        x = lax.rem(my_x + lax.div(j, 2), 4)
        y = lax.rem(my_y + lax.div(j, 8), 4)
        z = lax.rem(my_z + lax.div(j, 32), 4)
        return lax.div(z, 2) * 4 + y, lax.rem(z, 2) * 8 + x * 2 + c

    barrier = pltpu.get_barrier_semaphore()

    def greet(k, carry):
        pl.semaphore_signal(barrier, inc=1, device_id=target(k), device_id_type=MESH)
        return carry

    hbm_in = (k_hbm, v_hbm, g_hbm, q_hbm, h_hbm)
    K, V, G, Q, H = range(5)

    def load(n, g):
        cols = pl.ds(pl.multiple_of(g * width, width), width)
        return pltpu.make_async_copy(hbm_in[n].at[:, cols], ins.at[n, :, cols], load_sem.at[n, g])

    for g in range(GROUPS):
        for n in range(5):
            load(n, g).start()
    lax.fori_loop(1, DEVICES, greet, 0)

    def block_cols(g, b):
        return pl.ds(pl.multiple_of(g * width + b * 128, 128), 128)

    def prepare(g):
        for n in range(5):
            load(n, g).wait()

        def block(b, carry):
            cols = block_cols(g, b)
            rows = pl.ds(pl.multiple_of(b * 128, 128), 128)
            product = ins[K, :, cols].astype(F32) * ins[V, :, cols].astype(F32)
            gate = ins[G, :, cols].astype(F32) * ins[Q, :, cols].astype(F32)
            packed.reshape(GROUPS, 3, width, 128)[g, 0, rows, :] = product.astype(BF).T
            packed.reshape(GROUPS, 3, width, 128)[g, 1, rows, :] = gate.astype(BF).T
            packed.reshape(GROUPS, 3, width, 128)[g, 2, rows, :] = ins[H, :, cols].T
            return carry

        lax.fori_loop(0, width // 128, block, 0)

    def send_in(g):
        def one(k, carry):
            o, i = target(k)
            pltpu.make_async_remote_copy(
                src_ref=packed.at[g, :, pl.ds((o * 16 + i) * pairs, pairs)],
                dst_ref=held.at[g, :, :, pl.ds(me * 2, 2), :],
                send_sem=in_send,
                recv_sem=in_recv.at[g],
                device_id=(o, i),
                device_id_type=MESH,
            ).start()
            return carry

        pltpu.make_async_copy(
            packed.at[g, :, pl.ds(me * pairs, pairs)],
            held.at[g, :, :, pl.ds(me * 2, 2), :],
            in_recv.at[g],
        ).start()
        lax.fori_loop(1, DEVICES, one, 0)

    def send_out(g):
        def one(k, carry):
            o, i = target(k)
            pltpu.make_async_remote_copy(
                src_ref=made.at[g, :, :, pl.ds((o * 16 + i) * 2, 2), :],
                dst_ref=back.at[g, :, pl.ds(me * pairs, pairs)],
                send_sem=out_send,
                recv_sem=out_recv.at[g],
                device_id=(o, i),
                device_id_type=MESH,
            ).start()
            return carry

        pltpu.make_async_copy(
            made.at[g, :, :, pl.ds(me * 2, 2), :],
            back.at[g, :, pl.ds(me * pairs, pairs)],
            out_recv.at[g],
        ).start()
        lax.fori_loop(1, DEVICES, one, 0)

    def transform(g, h):
        wr, wi = tw_ref[0], tw_ref[1]
        pair = h * 2
        for n in range(3):
            rhs = jnp.concatenate([held[g, n, pair], held[g, n, pair + 1]], axis=1)
            one = jnp.dot(t1_ref[...], rhs, preferred_element_type=F32)
            for e in range(2):
                for p in range(2):
                    re = one[e * 256 : e * 256 + 128, p * 128 : p * 128 + 128]
                    im = one[e * 256 + 128 : e * 256 + 256, p * 128 : p * 128 + 128]
                    ch = p * 2 + e
                    part[n, ch, :, 0:128] = (re * wr + im * wi).astype(BF)
                    part[n, ch, :, 128:256] = (im * wr - re * wi).astype(BF)
        for ch in range(4):
            sp = []
            for n in range(3):
                sp.append(jnp.dot(part[n, ch], t2_ref[...], preferred_element_type=F32))
            vr, vi = sp[0][:, :128], sp[0][:, 128:]
            gr, gi = sp[1][:, :128], sp[1][:, 128:]
            fr, fi = sp[2][:, :128], sp[2][:, 128:]
            prods = (
                (vr * fr - vi * fi, vr * fi + vi * fr),
                (fr * gr + fi * gi, fr * gi - fi * gr),
                (vr * gr + vi * gi, vr * gi - vi * gr),
            )
            for n in range(3):
                qq = jnp.concatenate([prods[n][0].astype(BF), prods[n][1].astype(BF)], axis=1)
                three = jnp.dot(qq, t3_ref[...], preferred_element_type=F32)
                re, im = three[:, :128], three[:, 128:]
                p, e = ch // 2, ch % 2
                spec[n, e * 256 : e * 256 + 128, p * 128 : p * 128 + 128] = (
                    re * wr - im * wi
                ).astype(BF)
                spec[n, e * 256 + 128 : e * 256 + 256, p * 128 : p * 128 + 128] = (
                    im * wr + re * wi
                ).astype(BF)
        for n in range(3):
            four = jnp.dot(t4_ref[...], spec[n], preferred_element_type=F32)
            if n == 2:
                four = four * (1.0 / 128.0)
            for p in range(2):
                made[g, n, pair + p] = four[:, p * 128 : p * 128 + 128].astype(BF)

    lane = lax.broadcasted_iota(jnp.int32, (1, 128), 1)
    sub = lax.broadcasted_iota(jnp.int32, (8, 128), 0)

    def direct_sums(g):
        row = jnp.zeros((1, 128), F32)
        for p in range(pairs):
            terms = held[g, 0, p].astype(F32) * held[g, 1, p].astype(F32)
            folded = jnp.sum(terms.reshape(32, 8, 128), axis=0)
            for e in range(2):
                own = jnp.where(lax.rem(sub, 2) == e, folded, 0.0)
                total = jnp.sum(jnp.sum(own, axis=1, keepdims=True), axis=0, keepdims=True)
                row = row + jnp.where(lane == g * per + p * 2 + e, total, 0.0)
        sk_own[...] = sk_own[...] + row

    def send_sums():
        def one(k, carry):
            pltpu.make_async_remote_copy(
                src_ref=sk_own,
                dst_ref=sk_all.at[pl.ds(me, 1), :],
                send_sem=sk_send,
                recv_sem=sk_recv,
                device_id=target(k),
                device_id_type=MESH,
            ).start()
            return carry

        pltpu.make_async_copy(sk_own, sk_all.at[pl.ds(me, 1), :], sk_recv).start()
        lax.fori_loop(1, DEVICES, one, 0)

    def spread_sums():
        pltpu.make_async_copy(sk_all, sk_all, sk_recv).wait()
        rows = lax.broadcasted_iota(jnp.int32, (128, 128), 0)
        cols = lax.broadcasted_iota(jnp.int32, (128, 128), 1)
        mine = lax.div(cols, per) == lax.rem(rows, 16)
        for g in range(GROUPS):
            pick = (rows == g * per + lax.rem(cols, per)).astype(F32)
            wide = jnp.dot(
                sk_all[...], pick, preferred_element_type=F32, precision=lax.Precision.HIGHEST
            )
            kept = jnp.where(mine, wide, 0.0)
            sk_ref[g * 8 : g * 8 + 8, :] = jnp.sum(kept.reshape(8, 16, 128), axis=1) * (
                1.0 / 128.0
            )

    hbm_out = (lo_hbm, qg_hbm, kg_hbm, vg_hbm, fg_hbm)

    def store(n, g):
        cols = pl.ds(pl.multiple_of(g * width, width), width)
        return pltpu.make_async_copy(outs.at[n, :, cols], hbm_out[n].at[:, cols], store_sem.at[n, g])

    def finish(g):
        pltpu.make_async_copy(back.at[g], back.at[g], out_recv.at[g]).wait()

        def block(b, carry):
            cols = block_cols(g, b)
            rows = pl.ds(pl.multiple_of(b * 128, 128), 128)
            views = back.reshape(GROUPS, 3, width, 128)
            conv = views[g, 0, rows, :].T.astype(F32)
            corr = views[g, 1, rows, :].T.astype(F32)
            gain = gain_ref[pl.ds(g * (width // 128) + b, 1), :]
            kk, vv = ins[K, :, cols].astype(F32), ins[V, :, cols].astype(F32)
            gg, qq = ins[G, :, cols].astype(F32), ins[Q, :, cols].astype(F32)
            product = (kk * vv).astype(BF).astype(F32)
            mixing = conv + gain * product
            outs[0, :, cols] = (qq * mixing).astype(BF)
            outs[1, :, cols] = (gg * mixing).astype(BF)
            carried = corr + gain * (gg * qq)
            outs[2, :, cols] = (carried * vv).astype(BF)
            outs[3, :, cols] = (carried * kk).astype(BF)
            outs[4, :, cols] = views[g, 2, rows, :].T
            return carry

        lax.fori_loop(0, width // 128, block, 0)
        for n in range(5):
            store(n, g).start()

    sk_own[...] = jnp.zeros_like(sk_own)
    prepare(0)
    pl.semaphore_wait(barrier, DEVICES - 1)
    send_in(0)

    def ahead(g, carry):
        prepare(g)
        send_in(g)
        return carry

    lax.fori_loop(1, GROUPS, ahead, 0)

    def middle(g, carry):
        pltpu.make_async_copy(held.at[g], held.at[g], in_recv.at[g]).wait()

        def half(h, inside):
            transform(g, h)
            return inside

        lax.fori_loop(0, pairs // 2, half, 0)
        send_out(g)
        direct_sums(g)
        return carry

    lax.fori_loop(0, GROUPS, middle, 0)
    send_sums()

    def ending(g, carry):
        finish(g)
        return carry

    lax.fori_loop(0, GROUPS, ending, 0)
    spread_sums()
    everyone = held.at[:, :, :, pl.ds(0, 2 * (DEVICES - 1)), :]
    pltpu.make_async_copy(everyone, everyone, in_send).wait()
    pltpu.make_async_copy(everyone, everyone, out_send).wait()
    sums = sk_all.at[pl.ds(0, DEVICES - 1), :]
    pltpu.make_async_copy(sums, sums, sk_send).wait()
    for g in range(GROUPS):
        for n in range(5):
            store(n, g).wait()


def body(query_rows, key_rows, value_rows, out_grad, filter_rows, skip_gain):
    tokens, channels = query_rows.shape
    length = tokens * DEVICES
    width = channels // GROUPS
    per = width // DEVICES
    tables = [jnp.asarray(t) for t in coefficient_tables(tokens, DEVICES, length)]
    rows = jax.ShapeDtypeStruct((tokens, channels), BF)
    anywhere = pl.BlockSpec(memory_space=pl.ANY)
    vmem = pl.BlockSpec(memory_space=pltpu.VMEM)
    dma = pltpu.SemaphoreType.DMA
    results = pl.pallas_call(
        kernel,
        out_shape=[rows] * 5 + [jax.ShapeDtypeStruct((channels // 128, 128), F32)],
        in_specs=[anywhere] * 5 + [vmem] * 6,
        out_specs=[anywhere] * 5 + [vmem],
        scratch_shapes=[
            pltpu.VMEM((5, tokens, channels), BF),
            pltpu.VMEM((5, tokens, channels), BF),
            pltpu.VMEM((GROUPS, 3, width // 2, 2, 128), BF),
            pltpu.VMEM((GROUPS, 3, per // 2, 2 * DEVICES, 128), BF),
            pltpu.VMEM((GROUPS, 3, per // 2, 2 * DEVICES, 128), BF),
            pltpu.VMEM((GROUPS, 3, width // 2, 2, 128), BF),
            pltpu.VMEM((3, 4, DEVICES, 256), BF),
            pltpu.VMEM((3, 4 * DEVICES, 256), BF),
            pltpu.VMEM((1, 128), F32),
            pltpu.VMEM((DEVICES, 128), F32),
            dma((5, GROUPS)),
            dma((5, GROUPS)),
            dma,
            dma((GROUPS,)),
            dma,
            dma((GROUPS,)),
            dma,
            dma,
        ],
        compiler_params=pltpu.CompilerParams(
            collective_id=0, has_side_effects=True, vmem_limit_bytes=56 * 1024 * 1024
        ),
        name="hyena",
    )(
        query_rows,
        key_rows,
        value_rows,
        out_grad,
        filter_rows,
        skip_gain.reshape(channels // 128, 128),
        *tables,
    )
    return (*results[:5], results[5].reshape(channels))


def solution(mesh):
    rows = P(("outer", "inner"), None)
    return jax.shard_map(
        body,
        mesh=mesh,
        in_specs=(rows, rows, rows, rows, rows, P()),
        out_specs=(rows, rows, rows, rows, rows, P()),
        check_vma=False,
    )
```

time: 730 us -> 98.5 us (0.13)
  waiting for transfers between devices: 310 us -> 0 us
  local copies, waits for them, and re-layouts: 180 us -> 8.77 us
  Pallas kernels: 0 us -> 88.7 us
  blocking collectives: 81.8 us -> 0 us
  starting transfers between devices: 62.8 us -> 0 us
  other arithmetic: 59.3 us -> 0 us
  matrix products: 29 us -> 0 us
    all_to_all x8 -> x0, waiting for transfers between devices: 310 us -> none  [cut_exchange(): lax.all_to_all(slab, axis, split_axis=0, concat_axis=0, tiled=True)]
    pallas_call x0 -> x1, Pallas kernels: none -> 88.7 us  [body(): pl.pallas_call(kernel, out_shape=[rows] * 5 + [jax.ShapeDtypeStruct((chan...]
    psum x1 -> x0, blocking collectives: 81.8 us -> none  [body(): skip_sum = lax.psum(skip_part, ('outer', 'inner'))]
    all_to_all x8 -> x0, starting transfers between devices: 62.8 us -> none  [cut_exchange(): lax.all_to_all(slab, axis, split_axis=0, concat_axis=0, tiled=True)]
    split x13 -> x0, local copies, waits for them, and re-layouts: 62.5 us -> none  [cut_exchange(): jnp.split(tiles, cut_rows(tiles.shape[cut], pieces), axis=cut)]
    all_to_all x8 -> x0, local copies, waits for them, and re-layouts: 48.1 us -> none  [cut_exchange(): lax.all_to_all(slab, axis, split_axis=0, concat_axis=0, tiled=True)]
    dot_general x7 -> x0, matrix products: 29 us -> none  [the longest x2 11.1 us: body(): jnp.einsum('oisbc,iosjk->jkbc', section_one[:, :, half], table_two, prefe...]
    reshape x2 -> x0, other arithmetic: 25.1 us -> none  [the longest x1 18.4 us: in_blocks(): value.reshape(*dims[:dim], count, dims[dim] // count, *dims[dim + 1:])]
  transfers between devices with their start and end apart: 8 -> 0, of which waited for: 7 -> 0; matrix products, arithmetic and copies ran while one was open for 10% -> 0% of each run, Pallas kernels for 0% -> 0%
where the time goes in v1:
time: 98.5 us; the launch traced here: 98.2 us
  Pallas kernels  88.7 us (90%)
  local copies, waits for them, and re-layouts  8.77 us (9%)
    pallas_call x1, Pallas kernels, body(): pl.pallas_call(kernel, out_shape=[rows] * 5 + [jax.ShapeDtypeStruct((chan...  88.7 us
    unnamed x16, local copies, waits for them, and re-layouts  8.77 us

profile of v1, /device:TPU:1, one launch (start us, length us, event | category | flops | bytes accessed | tf_op | source)
XLA Modules:
  0.0 98.2 jit_solution(11411199388938578920)
XLA Ops:
  0.6 88.7 %hyena.1 = (bf16[128,4096]{1,0:T(8,128)(2,1)}, bf16[128,4096]{1,0:T(8,128)(2,1)}, bf16[128,4096]{1,0:T(8,128)(2,1)}, bf16[128,4096]{1,0:T(8,128)(2,1)}, bf16[128,4096]{1,0:T(8,128)(2,1)}, /*index=5*/f32[32,128]{1,0:T(8,128)}) custom-call(bf16[128,4096]{1,0:T(8,128)(2,1)} %q_hbm.1, bf16[128,4096]{1,0:T(8,128)(2,1)} %k_hbm.1, bf16[128,4096]{1,0:T(8,128)(2,1)} %v_hbm.1, ...), custom_call_target="tpu_custom_call" | custom-call | tf_op jit(solution)/shard_map/hyena/pallas_call | solution.py:351
  89.4 0.0 copy-start.3
  89.4 2.4 %copy.23 = bf16[128,4096]{1,0:T(8,128)(2,1)} copy(bf16[128,4096]{1,0:T(8,128)(2,1)} %get-tuple-element.24) | data formatting | bytes 2097152
  91.8 0.0 copy-done.3
  91.8 0.0 copy-start.2
  91.8 1.0 copy.24
  92.7 0.6 copy-done.2
  93.4 0.0 copy-start.1
  93.4 1.0 copy.25
  94.3 0.6 copy-done.1
  95.0 0.0 copy-start
  95.0 1.0 copy.26
  95.9 0.6 copy-done
  96.6 0.0 copy-start.4
  96.6 1.0 copy.27
  97.6 0.0 copy-done.4
  97.6 0.6 copy.28
Async XLA Ops:
  89.4 2.4 %copy-start.3 = (bf16[128,4096]{1,0:T(8,128)(2,1)S(1)}, bf16[128,4096]{1,0:T(8,128)(2,1)}, u32[]{:S(2)}) copy-start(bf16[128,4096]{1,0:T(8,128)(2,1)} %get-tuple-element.25) | copy-start | bytes 3145732
  91.8 1.6 %copy-start.2 = (bf16[128,4096]{1,0:T(8,128)(2,1)S(1)}, bf16[128,4096]{1,0:T(8,128)(2,1)}, u32[]{:S(2)}) copy-start(bf16[128,4096]{1,0:T(8,128)(2,1)} %get-tuple-element.26) | copy-start | bytes 3145732
  93.4 1.6 %copy-start.1 = (bf16[128,4096]{1,0:T(8,128)(2,1)S(1)}, bf16[128,4096]{1,0:T(8,128)(2,1)}, u32[]{:S(2)}) copy-start(bf16[128,4096]{1,0:T(8,128)(2,1)} %get-tuple-element.27) | copy-start | bytes 3145732
  95.0 1.6 %copy-start = (bf16[128,4096]{1,0:T(8,128)(2,1)S(1)}, bf16[128,4096]{1,0:T(8,128)(2,1)}, u32[]{:S(2)}) copy-start(bf16[128,4096]{1,0:T(8,128)(2,1)} %get-tuple-element.28) | copy-start | bytes 3145732
  96.6 1.0 copy-start.4

commit v2 on v1

--- a/solution.py
+++ b/solution.py
@@ -49,17 +49,24 @@
     v_hbm,
     g_hbm,
     h_hbm,
+    gain_hbm,
+    t1_hbm,
+    t2_hbm,
+    t3_hbm,
+    t4_hbm,
+    tw_hbm,
+    lo_hbm,
+    qg_hbm,
+    kg_hbm,
+    vg_hbm,
+    fg_hbm,
+    sk_hbm,
     gain_ref,
     t1_ref,
     t2_ref,
     t3_ref,
     t4_ref,
     tw_ref,
-    lo_hbm,
-    qg_hbm,
-    kg_hbm,
-    vg_hbm,
-    fg_hbm,
     sk_ref,
     ins,
     outs,
@@ -72,6 +79,7 @@
     sk_own,
     sk_all,
     load_sem,
+    table_sem,
     store_sem,
     in_send,
     in_recv,
@@ -100,10 +108,22 @@
         return lax.div(z, 2) * 4 + y, lax.rem(z, 2) * 8 + x * 2 + c
 
     barrier = pltpu.get_barrier_semaphore()
-
-    def greet(k, carry):
-        pl.semaphore_signal(barrier, inc=1, device_id=target(k), device_id_type=MESH)
-        return carry
+    row = my_x * 2 + my_c
+
+    def greet():
+        for dz in (2, 1, 3, 0):
+            z = lax.rem(my_z + dz, 4)
+            for dy in (2, 1, 3, 0):
+                o = lax.div(z, 2) * 4 + lax.rem(my_y + dy, 4)
+                base = lax.rem(z, 2) * 8
+                alone = dz == 0 and dy == 0
+
+                def one(t, carry):
+                    i = base + (lax.rem(row + t, 8) if alone else t)
+                    pl.semaphore_signal(barrier, inc=1, device_id=(o, i), device_id_type=MESH)
+                    return carry
+
+                lax.fori_loop(1 if alone else 0, 8, one, 0)
 
     hbm_in = (k_hbm, v_hbm, g_hbm, q_hbm, h_hbm)
     K, V, G, Q, H = range(5)
@@ -112,10 +132,22 @@
         cols = pl.ds(pl.multiple_of(g * width, width), width)
         return pltpu.make_async_copy(hbm_in[n].at[:, cols], ins.at[n, :, cols], load_sem.at[n, g])
 
-    for g in range(GROUPS):
+    for n in range(5):
+        load(n, 0).start()
+    greet()
+    for g in range(1, GROUPS):
         for n in range(5):
             load(n, g).start()
-    lax.fori_loop(1, DEVICES, greet, 0)
+    fixed = (
+        (t1_hbm, t1_ref),
+        (t2_hbm, t2_ref),
+        (t3_hbm, t3_ref),
+        (t4_hbm, t4_ref),
+        (tw_hbm, tw_ref),
+        (gain_hbm, gain_ref),
+    )
+    for n, (source, place) in enumerate(fixed):
+        pltpu.make_async_copy(source, place, table_sem.at[n]).start()
 
     def block_cols(g, b):
         return pl.ds(pl.multiple_of(g * width + b * 128, 128), 128)
@@ -307,6 +339,9 @@
 
     lax.fori_loop(1, GROUPS, ahead, 0)
 
+    for n, (source, place) in enumerate(fixed):
+        pltpu.make_async_copy(source, place, table_sem.at[n]).wait()
+
     def middle(g, carry):
         pltpu.make_async_copy(held.at[g], held.at[g], in_recv.at[g]).wait()
 
@@ -326,8 +361,11 @@
         finish(g)
         return carry
 
-    lax.fori_loop(0, GROUPS, ending, 0)
+    lax.fori_loop(0, GROUPS - 1, ending, 0)
     spread_sums()
+    finish(GROUPS - 1)
+    sums_out = pltpu.make_async_copy(sk_ref, sk_hbm, table_sem.at[0])
+    sums_out.start()
     everyone = held.at[:, :, :, pl.ds(0, 2 * (DEVICES - 1)), :]
     pltpu.make_async_copy(everyone, everyone, in_send).wait()
     pltpu.make_async_copy(everyone, everyone, out_send).wait()
@@ -336,6 +374,19 @@
     for g in range(GROUPS):
         for n in range(5):
             store(n, g).wait()
+    sums_out.wait()
+
+
+def deliver(*refs):
+    count = len(refs) // 2
+    sem = refs[-1]
+    copies = [
+        pltpu.make_async_copy(refs[n], refs[count + n], sem.at[n]) for n in range(count)
+    ]
+    for copy in copies:
+        copy.start()
+    for copy in copies:
+        copy.wait()
 
 
 def body(query_rows, key_rows, value_rows, out_grad, filter_rows, skip_gain):
@@ -346,14 +397,18 @@
     tables = [jnp.asarray(t) for t in coefficient_tables(tokens, DEVICES, length)]
     rows = jax.ShapeDtypeStruct((tokens, channels), BF)
     anywhere = pl.BlockSpec(memory_space=pl.ANY)
-    vmem = pl.BlockSpec(memory_space=pltpu.VMEM)
     dma = pltpu.SemaphoreType.DMA
+    shapes = [rows] * 5 + [jax.ShapeDtypeStruct((channels // 128, 128), F32)]
+    hbm = pl.BlockSpec(memory_space=pltpu.HBM)
     results = pl.pallas_call(
         kernel,
-        out_shape=[rows] * 5 + [jax.ShapeDtypeStruct((channels // 128, 128), F32)],
-        in_specs=[anywhere] * 5 + [vmem] * 6,
-        out_specs=[anywhere] * 5 + [vmem],
+        out_shape=shapes,
+        in_specs=[hbm] * 11,
+        out_specs=[anywhere] * 6,
         scratch_shapes=[
+            pltpu.VMEM((channels // 128, 128), F32),
+            *[pltpu.VMEM(t.shape, t.dtype) for t in tables],
+            pltpu.VMEM((channels // 128, 128), F32),
             pltpu.VMEM((5, tokens, channels), BF),
             pltpu.VMEM((5, tokens, channels), BF),
             pltpu.VMEM((GROUPS, 3, width // 2, 2, 128), BF),
@@ -365,6 +420,7 @@
             pltpu.VMEM((1, 128), F32),
             pltpu.VMEM((DEVICES, 128), F32),
             dma((5, GROUPS)),
+            dma((6,)),
             dma((5, GROUPS)),
             dma,
             dma((GROUPS,)),
@@ -374,18 +430,32 @@
             dma,
         ],
         compiler_params=pltpu.CompilerParams(
-            collective_id=0, has_side_effects=True, vmem_limit_bytes=56 * 1024 * 1024
+            collective_id=0, has_side_effects=True, vmem_limit_bytes=36 * 1024 * 1024
         ),
         name="hyena",
     )(
-        query_rows,
-        key_rows,
-        value_rows,
-        out_grad,
-        filter_rows,
-        skip_gain.reshape(channels // 128, 128),
-        *tables,
+        *(
+            pltpu.with_memory_space_constraint(a, pltpu.HBM)
+            for a in (
+                query_rows,
+                key_rows,
+                value_rows,
+                out_grad,
+                filter_rows,
+                skip_gain.reshape(channels // 128, 128),
+                *tables,
+            )
+        )
     )
+    results = pl.pallas_call(
+        deliver,
+        out_shape=shapes,
+        in_specs=[anywhere] * 6,
+        out_specs=[hbm] * 6,
+        scratch_shapes=[dma((6,))],
+        compiler_params=pltpu.CompilerParams(vmem_limit_bytes=1024 * 1024),
+        name="deliver",
+    )(*results)
     return (*results[:5], results[5].reshape(channels))
 
 

time: 98.5 us -> 88.1 us (0.89)
  local copies, waits for them, and re-layouts: 8.77 us -> 0 us
  Pallas kernels: 88.7 us -> 87.4 us
    unnamed x16 -> x0, local copies, waits for them, and re-layouts: 8.77 us -> none
    pallas_call x1 -> x2, Pallas kernels: 88.7 us -> 87.4 us  [the longest x1 85 us: body(): pl.pallas_call(kernel, out_shape=shapes, in_specs=[hbm] * 11, out_specs=[...]
where the time goes in v2:
time: 88.1 us; the launch traced here: 88 us
  Pallas kernels  87.4 us (99%)
    pallas_call x1, Pallas kernels, body(): pl.pallas_call(kernel, out_shape=shapes, in_specs=[hbm] * 11, out_specs=[...  85 us
    pallas_call x1, Pallas kernels, body(): pl.pallas_call(deliver, out_shape=shapes, in_specs=[anywhere] * 6, out_sp...  2.41 us

profile of v2, /device:TPU:1, one launch (start us, length us, event | category | flops | bytes accessed | tf_op | source)
XLA Modules:
  0.0 88.0 jit_solution(17971791135616511084)
XLA Ops:
  0.6 85.0 %hyena.1 = (bf16[128,4096]{1,0:T(8,128)(2,1)S(1)}, bf16[128,4096]{1,0:T(8,128)(2,1)S(1)}, bf16[128,4096]{1,0:T(8,128)(2,1)S(1)}, bf16[128,4096]{1,0:T(8,128)(2,1...) custom-call(bf16[128,4096]{1,0:T(8,128)(2,1)} %q_hbm.1, bf16[128,4096]{1,0:T(8,128)(2,1)} %k_hbm.1, ...), custom_call_target="tpu_custom_call" | custom-call | tf_op jit(solution)/shard_map/hyena/pallas_call | solution.py:403
  85.6 2.4 %deliver.1 = (bf16[128,4096]{1,0:T(8,128)(2,1)}, bf16[128,4096]{1,0:T(8,128)(2,1)}, bf16[128,4096]{1,0:T(8,128)(2,1)}, bf16[128,4096]{1,0:T(8,128)(2,1)}, bf16[128,4096]{1,0:T(8,128)(2,1)}, /*index=5*/f32[32,128]{1,0:T(8,128)}) custom-call(bf16[128,4096]{1,0:T(8,128)(2,1)S(1)} %get-tuple-element.18.refs_0_, bf16[128,4096]{1,0:T(8,128)(2,1)S(1)} %get-tuple-element.19.refs_1_, ...), custom_call_target="tpu_custom_call" | custom-call | tf_op jit(solution)/shard_map/deliver/pallas_call | solution.py:450

commit v3 on v2

--- a/solution.py
+++ b/solution.py
@@ -15,6 +15,8 @@
 DEVICES = 128
 GROUPS = 4
 ORDER = 91
+VMEM_MAIN = 40
+VMEM_LAST = 16
 
 
 def coefficient_tables(tokens, devices, length):
@@ -55,21 +57,20 @@
     t3_hbm,
     t4_hbm,
     tw_hbm,
-    lo_hbm,
-    qg_hbm,
-    kg_hbm,
-    vg_hbm,
-    fg_hbm,
-    sk_hbm,
+    lo_ref,
+    qg_ref,
+    kg_ref,
+    vg_ref,
+    fg_ref,
+    ins,
+    final,
     gain_ref,
+    sk_ref,
     t1_ref,
     t2_ref,
     t3_ref,
     t4_ref,
     tw_ref,
-    sk_ref,
-    ins,
-    outs,
     packed,
     held,
     made,
@@ -80,7 +81,6 @@
     sk_all,
     load_sem,
     table_sem,
-    store_sem,
     in_send,
     in_recv,
     out_send,
@@ -113,17 +113,13 @@
     def greet():
         for dz in (2, 1, 3, 0):
             z = lax.rem(my_z + dz, 4)
+            base = lax.rem(z, 2) * 8
             for dy in (2, 1, 3, 0):
                 o = lax.div(z, 2) * 4 + lax.rem(my_y + dy, 4)
-                base = lax.rem(z, 2) * 8
                 alone = dz == 0 and dy == 0
-
-                def one(t, carry):
+                for t in range(1 if alone else 0, 8):
                     i = base + (lax.rem(row + t, 8) if alone else t)
                     pl.semaphore_signal(barrier, inc=1, device_id=(o, i), device_id_type=MESH)
-                    return carry
-
-                lax.fori_loop(1 if alone else 0, 8, one, 0)
 
     hbm_in = (k_hbm, v_hbm, g_hbm, q_hbm, h_hbm)
     K, V, G, Q, H = range(5)
@@ -188,12 +184,12 @@
         ).start()
         lax.fori_loop(1, DEVICES, one, 0)
 
-    def send_out(g):
+    def send_out(g, place):
         def one(k, carry):
             o, i = target(k)
             pltpu.make_async_remote_copy(
                 src_ref=made.at[g, :, :, pl.ds((o * 16 + i) * 2, 2), :],
-                dst_ref=back.at[g, :, pl.ds(me * pairs, pairs)],
+                dst_ref=place.at[:, pl.ds(me * pairs, pairs)],
                 send_sem=out_send,
                 recv_sem=out_recv.at[g],
                 device_id=(o, i),
@@ -203,7 +199,7 @@
 
         pltpu.make_async_copy(
             made.at[g, :, :, pl.ds(me * 2, 2), :],
-            back.at[g, :, pl.ds(me * pairs, pairs)],
+            place.at[:, pl.ds(me * pairs, pairs)],
             out_recv.at[g],
         ).start()
         lax.fori_loop(1, DEVICES, one, 0)
@@ -295,11 +291,7 @@
                 1.0 / 128.0
             )
 
-    hbm_out = (lo_hbm, qg_hbm, kg_hbm, vg_hbm, fg_hbm)
-
-    def store(n, g):
-        cols = pl.ds(pl.multiple_of(g * width, width), width)
-        return pltpu.make_async_copy(outs.at[n, :, cols], hbm_out[n].at[:, cols], store_sem.at[n, g])
+    outs = (lo_ref, qg_ref, kg_ref, vg_ref, fg_ref)
 
     def finish(g):
         pltpu.make_async_copy(back.at[g], back.at[g], out_recv.at[g]).wait()
@@ -307,25 +299,17 @@
         def block(b, carry):
             cols = block_cols(g, b)
             rows = pl.ds(pl.multiple_of(b * 128, 128), 128)
-            views = back.reshape(GROUPS, 3, width, 128)
-            conv = views[g, 0, rows, :].T.astype(F32)
-            corr = views[g, 1, rows, :].T.astype(F32)
-            gain = gain_ref[pl.ds(g * (width // 128) + b, 1), :]
-            kk, vv = ins[K, :, cols].astype(F32), ins[V, :, cols].astype(F32)
-            gg, qq = ins[G, :, cols].astype(F32), ins[Q, :, cols].astype(F32)
-            product = (kk * vv).astype(BF).astype(F32)
-            mixing = conv + gain * product
-            outs[0, :, cols] = (qq * mixing).astype(BF)
-            outs[1, :, cols] = (gg * mixing).astype(BF)
-            carried = corr + gain * (gg * qq)
-            outs[2, :, cols] = (carried * vv).astype(BF)
-            outs[3, :, cols] = (carried * kk).astype(BF)
-            outs[4, :, cols] = views[g, 2, rows, :].T
+            views = back.reshape(GROUPS - 1, 3, width, 128)
+            results = results_of(
+                [views[g, n, rows, :] for n in range(3)],
+                [ins[n, :, cols] for n in range(4)],
+                gain_ref[pl.ds(g * (width // 128) + b, 1), :],
+            )
+            for n in range(5):
+                outs[n][:, cols] = results[n]
             return carry
 
         lax.fori_loop(0, width // 128, block, 0)
-        for n in range(5):
-            store(n, g).start()
 
     sk_own[...] = jnp.zeros_like(sk_own)
     prepare(0)
@@ -349,13 +333,25 @@
             transform(g, h)
             return inside
 
+        direct_sums(g)
+
+        @pl.when(g == GROUPS - 1)
+        def _():
+            send_sums()
+
         lax.fori_loop(0, pairs // 2, half, 0)
-        send_out(g)
-        direct_sums(g)
+
+        @pl.when(g < GROUPS - 1)
+        def _():
+            send_out(g, back.at[g])
+
+        @pl.when(g == GROUPS - 1)
+        def _():
+            send_out(g, final)
+
         return carry
 
     lax.fori_loop(0, GROUPS, middle, 0)
-    send_sums()
 
     def ending(g, carry):
         finish(g)
@@ -363,28 +359,70 @@
 
     lax.fori_loop(0, GROUPS - 1, ending, 0)
     spread_sums()
-    finish(GROUPS - 1)
-    sums_out = pltpu.make_async_copy(sk_ref, sk_hbm, table_sem.at[0])
-    sums_out.start()
     everyone = held.at[:, :, :, pl.ds(0, 2 * (DEVICES - 1)), :]
     pltpu.make_async_copy(everyone, everyone, in_send).wait()
-    pltpu.make_async_copy(everyone, everyone, out_send).wait()
     sums = sk_all.at[pl.ds(0, DEVICES - 1), :]
     pltpu.make_async_copy(sums, sums, sk_send).wait()
-    for g in range(GROUPS):
-        for n in range(5):
-            store(n, g).wait()
-    sums_out.wait()
+    pltpu.make_async_copy(final, final, out_recv.at[GROUPS - 1]).wait()
+    pltpu.make_async_copy(everyone, everyone, out_send).wait()
+
+
+def results_of(sums, rows, gain):
+    conv, corr = sums[0].T.astype(F32), sums[1].T.astype(F32)
+    kk, vv, gg, qq = (r.astype(F32) for r in rows)
+    product = (kk * vv).astype(BF).astype(F32)
+    mixing = conv + gain * product
+    carried = corr + gain * (gg * qq)
+    return (
+        (qq * mixing).astype(BF),
+        (gg * mixing).astype(BF),
+        (carried * vv).astype(BF),
+        (carried * kk).astype(BF),
+        sums[2].T,
+    )
 
 
 def deliver(*refs):
-    count = len(refs) // 2
-    sem = refs[-1]
+    early, (ins, final, gain_ref, sums) = refs[:5], refs[5:9]
+    whole, sums_out = refs[9:14], refs[14]
+    late, sem = refs[15], refs[16]
+    channels = whole[0].shape[1]
+    width = channels // GROUPS
+    first = channels - width
+    parts = 2
+    step = width // parts
     copies = [
-        pltpu.make_async_copy(refs[n], refs[count + n], sem.at[n]) for n in range(count)
+        pltpu.make_async_copy(early[n], whole[n].at[:, pl.ds(0, first)], sem.at[n])
+        for n in range(5)
     ]
+    copies.append(pltpu.make_async_copy(sums, sums_out, sem.at[5]))
     for copy in copies:
         copy.start()
+    views = final.reshape(3, width, 128)
+    for part in range(parts):
+
+        def block(b, carry):
+            at = pl.multiple_of(part * step + b * 128, 128)
+            cols = pl.ds(first + at, 128)
+            results = results_of(
+                [views[n, pl.ds(at, 128), :] for n in range(3)],
+                [ins[n, :, cols] for n in range(4)],
+                gain_ref[pl.ds((first + part * step) // 128 + b, 1), :],
+            )
+            for n in range(5):
+                late[n, :, pl.ds(at, 128)] = results[n]
+            return carry
+
+        lax.fori_loop(0, step // 128, block, 0)
+        for n in range(5):
+            copies.append(
+                pltpu.make_async_copy(
+                    late.at[n, :, pl.ds(part * step, step)],
+                    whole[n].at[:, pl.ds(first + part * step, step)],
+                    sem.at[6 + part * 5 + n],
+                )
+            )
+            copies[-1].start()
     for copy in copies:
         copy.wait()
 
@@ -398,30 +436,33 @@
     rows = jax.ShapeDtypeStruct((tokens, channels), BF)
     anywhere = pl.BlockSpec(memory_space=pl.ANY)
     dma = pltpu.SemaphoreType.DMA
-    shapes = [rows] * 5 + [jax.ShapeDtypeStruct((channels // 128, 128), F32)]
+    sums = jax.ShapeDtypeStruct((channels // 128, 128), F32)
+    early = jax.ShapeDtypeStruct((tokens, channels - width), BF)
     hbm = pl.BlockSpec(memory_space=pltpu.HBM)
-    results = pl.pallas_call(
+    vmem = pl.BlockSpec(memory_space=pltpu.VMEM)
+    handed = pl.pallas_call(
         kernel,
-        out_shape=shapes,
+        out_shape=[early] * 5
+        + [
+            jax.ShapeDtypeStruct((5, tokens, channels), BF),
+            jax.ShapeDtypeStruct((3, width // 2, 2, 128), BF),
+            sums,
+            sums,
+        ],
         in_specs=[hbm] * 11,
-        out_specs=[anywhere] * 6,
+        out_specs=[vmem] * 9,
         scratch_shapes=[
-            pltpu.VMEM((channels // 128, 128), F32),
             *[pltpu.VMEM(t.shape, t.dtype) for t in tables],
-            pltpu.VMEM((channels // 128, 128), F32),
-            pltpu.VMEM((5, tokens, channels), BF),
-            pltpu.VMEM((5, tokens, channels), BF),
             pltpu.VMEM((GROUPS, 3, width // 2, 2, 128), BF),
             pltpu.VMEM((GROUPS, 3, per // 2, 2 * DEVICES, 128), BF),
             pltpu.VMEM((GROUPS, 3, per // 2, 2 * DEVICES, 128), BF),
-            pltpu.VMEM((GROUPS, 3, width // 2, 2, 128), BF),
+            pltpu.VMEM((GROUPS - 1, 3, width // 2, 2, 128), BF),
             pltpu.VMEM((3, 4, DEVICES, 256), BF),
             pltpu.VMEM((3, 4 * DEVICES, 256), BF),
             pltpu.VMEM((1, 128), F32),
             pltpu.VMEM((DEVICES, 128), F32),
             dma((5, GROUPS)),
             dma((6,)),
-            dma((5, GROUPS)),
             dma,
             dma((GROUPS,)),
             dma,
@@ -430,7 +471,7 @@
             dma,
         ],
         compiler_params=pltpu.CompilerParams(
-            collective_id=0, has_side_effects=True, vmem_limit_bytes=36 * 1024 * 1024
+            collective_id=0, has_side_effects=True, vmem_limit_bytes=VMEM_MAIN * 1024 * 1024
         ),
         name="hyena",
     )(
@@ -449,13 +490,13 @@
     )
     results = pl.pallas_call(
         deliver,
-        out_shape=shapes,
-        in_specs=[anywhere] * 6,
+        out_shape=[rows] * 5 + [sums],
+        in_specs=[anywhere] * 5 + [vmem] * 3 + [anywhere],
         out_specs=[hbm] * 6,
-        scratch_shapes=[dma((6,))],
-        compiler_params=pltpu.CompilerParams(vmem_limit_bytes=1024 * 1024),
+        scratch_shapes=[pltpu.VMEM((5, tokens, width), BF), dma((16,))],
+        compiler_params=pltpu.CompilerParams(vmem_limit_bytes=VMEM_LAST * 1024 * 1024),
         name="deliver",
-    )(*results)
+    )(*handed)
     return (*results[:5], results[5].reshape(channels))
 
 

time: 88.1 us -> 85.5 us (0.970)
  Pallas kernels: 87.4 us -> 84.8 us
    pallas_call x2, Pallas kernels: 87.4 us -> 84.8 us  [the longest x1 82.3 us: body(): pl.pallas_call(kernel, out_shape=[early] * 5 + [jax.ShapeDtypeStruct((5,...]
where the time goes in v3:
time: 85.5 us; the launch traced here: 85.4 us
  Pallas kernels  84.8 us (99%)
    pallas_call x1, Pallas kernels, body(): pl.pallas_call(kernel, out_shape=[early] * 5 + [jax.ShapeDtypeStruct((5,...  82.3 us
    pallas_call x1, Pallas kernels, body(): pl.pallas_call(deliver, out_shape=[rows] * 5 + [sums], in_specs=[anywhere...  2.46 us

profile of v3, /device:TPU:1, one launch (start us, length us, event | category | flops | bytes accessed | tf_op | source)
XLA Modules:
  0.0 85.4 jit_solution(1218554163155596229)
XLA Ops:
  0.6 82.3 %hyena.1 = (bf16[128,3072]{1,0:T(8,128)(2,1)S(1)}, bf16[128,3072]{1,0:T(8,128)(2,1)S(1)}, bf16[128,3072]{1,0:T(8,128)(2,1)S(1)}, bf16[128,3072]{1,0:T(8,128)(2,1...) custom-call(bf16[128,4096]{1,0:T(8,128)(2,1)} %q_hbm.1, ...), custom_call_target="tpu_custom_call" | custom-call | tf_op jit(solution)/shard_map/hyena/pallas_call | solution.py:443
  83.0 2.5 %deliver.1 = (bf16[128,4096]{1,0:T(8,128)(2,1)}, bf16[128,4096]{1,0:T(8,128)(2,1)}, bf16[128,4096]{1,0:T(8,128)(2,1)}, bf16[128,4096]{1,0:T(8,128)(2,1)}, bf16[128,4096]{1,0:T(8,128)(2,1)}, /*index=5*/f32[32,128]{1,0:T(8,128)}) custom-call(bf16[128,3072]{1,0:T(8,128)(2,1)S(1)} %get-tuple-element.21.refs_0_, bf16[128,3072]{1,0:T(8,128)(2,1)S(1)} %get-tuple-element.22.refs_1_, ...), custom_call_target="tpu_custom_call" | custom-call | tf_op jit(solution)/shard_map/deliver/pallas_call | solution.py:491

commit v4 on v3

--- a/solution.py
+++ b/solution.py
@@ -78,6 +78,8 @@
     part,
     spec,
     sk_own,
+    sk_near,
+    sk_row,
     sk_all,
     load_sem,
     table_sem,
@@ -87,6 +89,8 @@
     out_recv,
     sk_send,
     sk_recv,
+    near_send,
+    near_recv,
 ):
     tokens, channels = q_hbm.shape
     width = channels // GROUPS
@@ -184,7 +188,14 @@
         ).start()
         lax.fori_loop(1, DEVICES, one, 0)
 
-    def send_out(g, place):
+    def hops(k):
+        j = lax.rem(k * ORDER, DEVICES)
+        total = 0
+        for d in (lax.rem(lax.div(j, 2), 4), lax.rem(lax.div(j, 8), 4), lax.div(j, 32)):
+            total = total + jnp.minimum(d, 4 - d)
+        return total
+
+    def send_out(g, place, far_first=False):
         def one(k, carry):
             o, i = target(k)
             pltpu.make_async_remote_copy(
@@ -197,12 +208,30 @@
             ).start()
             return carry
 
+        def far(k, carry):
+            @pl.when(hops(k) > 2)
+            def _():
+                one(k, 0)
+
+            return carry
+
+        def near(k, carry):
+            @pl.when(hops(k) <= 2)
+            def _():
+                one(k, 0)
+
+            return carry
+
         pltpu.make_async_copy(
             made.at[g, :, :, pl.ds(me * 2, 2), :],
             place.at[:, pl.ds(me * pairs, pairs)],
             out_recv.at[g],
         ).start()
-        lax.fori_loop(1, DEVICES, one, 0)
+        if far_first:
+            lax.fori_loop(1, DEVICES, far, 0)
+            lax.fori_loop(1, DEVICES, near, 0)
+        else:
+            lax.fori_loop(1, DEVICES, one, 0)
 
     def transform(g, h):
         wr, wi = tw_ref[0], tw_ref[1]
@@ -262,32 +291,57 @@
         sk_own[...] = sk_own[...] + row
 
     def send_sums():
-        def one(k, carry):
+        own = sk_own[...]
+        spread = own
+        for n in range(1, 4):
+            spread = jnp.where(lax.div(lane, per * GROUPS) == n, pltpu.roll(own, n * per * GROUPS, 1), spread)
+        sk_own[...] = jnp.where(lax.div(lane, per * GROUPS) == lax.rem(row, 4), spread, 0.0)
+        pltpu.make_async_copy(sk_own, sk_near.at[pl.ds(row, 1), :], near_recv).start()
+        for t in range(1, 8):
             pltpu.make_async_remote_copy(
                 src_ref=sk_own,
-                dst_ref=sk_all.at[pl.ds(me, 1), :],
-                send_sem=sk_send,
-                recv_sem=sk_recv,
-                device_id=target(k),
+                dst_ref=sk_near.at[pl.ds(row, 1), :],
+                send_sem=near_send,
+                recv_sem=near_recv,
+                device_id=(outer, my_zl * 8 + lax.rem(row + t, 8)),
                 device_id_type=MESH,
             ).start()
-            return carry
-
-        pltpu.make_async_copy(sk_own, sk_all.at[pl.ds(me, 1), :], sk_recv).start()
-        lax.fori_loop(1, DEVICES, one, 0)
+
+    def pass_sums():
+        pltpu.make_async_copy(sk_near, sk_near, near_recv).wait()
+        sk_row[...] = jnp.sum(sk_near[...].reshape(2, 4, 128), axis=1)
+        mine = outer * 2 + my_zl
+        pltpu.make_async_copy(sk_row, sk_all.at[mine], sk_recv).start()
+        for dz in (2, 1, 3, 0):
+            z = lax.rem(my_z + dz, 4)
+            for dy in (2, 1, 3, 0):
+                if dz or dy:
+                    o = lax.div(z, 2) * 4 + lax.rem(my_y + dy, 4)
+                    pltpu.make_async_remote_copy(
+                        src_ref=sk_row,
+                        dst_ref=sk_all.at[mine],
+                        send_sem=sk_send,
+                        recv_sem=sk_recv,
+                        device_id=(o, lax.rem(z, 2) * 8 + row),
+                        device_id_type=MESH,
+                    ).start()
 
     def spread_sums():
         pltpu.make_async_copy(sk_all, sk_all, sk_recv).wait()
-        rows = lax.broadcasted_iota(jnp.int32, (128, 128), 0)
-        cols = lax.broadcasted_iota(jnp.int32, (128, 128), 1)
-        mine = lax.div(cols, per) == lax.rem(rows, 16)
+        gathered = sk_all[...].reshape(32, 128)
+        rows = lax.broadcasted_iota(jnp.int32, (32, 128), 0)
+        cols = lax.broadcasted_iota(jnp.int32, (32, 128), 1)
+        mine = lax.div(cols, 32) == lax.rem(rows, 4)
+        source = lax.broadcasted_iota(jnp.int32, (128, 128), 0)
+        place = lax.broadcasted_iota(jnp.int32, (128, 128), 1)
+        base = lax.rem(lax.div(place, per), 4) * (per * GROUPS) + lax.rem(place, per)
         for g in range(GROUPS):
-            pick = (rows == g * per + lax.rem(cols, per)).astype(F32)
+            pick = (source == base + g * per).astype(F32)
             wide = jnp.dot(
-                sk_all[...], pick, preferred_element_type=F32, precision=lax.Precision.HIGHEST
+                gathered, pick, preferred_element_type=F32, precision=lax.Precision.HIGHEST
             )
             kept = jnp.where(mine, wide, 0.0)
-            sk_ref[g * 8 : g * 8 + 8, :] = jnp.sum(kept.reshape(8, 16, 128), axis=1) * (
+            sk_ref[g * 8 : g * 8 + 8, :] = jnp.sum(kept.reshape(8, 4, 128), axis=1) * (
                 1.0 / 128.0
             )
 
@@ -347,7 +401,7 @@
 
         @pl.when(g == GROUPS - 1)
         def _():
-            send_out(g, final)
+            send_out(g, final, far_first=True)
 
         return carry
 
@@ -357,11 +411,15 @@
         finish(g)
         return carry
 
-    lax.fori_loop(0, GROUPS - 1, ending, 0)
+    lax.fori_loop(0, GROUPS - 2, ending, 0)
+    pass_sums()
+    finish(GROUPS - 2)
     spread_sums()
     everyone = held.at[:, :, :, pl.ds(0, 2 * (DEVICES - 1)), :]
     pltpu.make_async_copy(everyone, everyone, in_send).wait()
-    sums = sk_all.at[pl.ds(0, DEVICES - 1), :]
+    near = sk_near.at[pl.ds(0, 7), :]
+    pltpu.make_async_copy(near, near, near_send).wait()
+    sums = sk_all.at[pl.ds(0, 15)]
     pltpu.make_async_copy(sums, sums, sk_send).wait()
     pltpu.make_async_copy(final, final, out_recv.at[GROUPS - 1]).wait()
     pltpu.make_async_copy(everyone, everyone, out_send).wait()
@@ -460,13 +518,17 @@
             pltpu.VMEM((3, 4, DEVICES, 256), BF),
             pltpu.VMEM((3, 4 * DEVICES, 256), BF),
             pltpu.VMEM((1, 128), F32),
-            pltpu.VMEM((DEVICES, 128), F32),
+            pltpu.VMEM((8, 128), F32),
+            pltpu.VMEM((2, 128), F32),
+            pltpu.VMEM((16, 2, 128), F32),
             dma((5, GROUPS)),
             dma((6,)),
             dma,
             dma((GROUPS,)),
             dma,
             dma((GROUPS,)),
+            dma,
+            dma,
             dma,
             dma,
         ],

time: 85.5 us -> 85.5 us (level)
  no operation moved by 1% of the time
where the time goes in v4:
time: 85.5 us; the launch traced here: 85.4 us
  Pallas kernels  84.7 us (99%)
    pallas_call x1, Pallas kernels, body(): pl.pallas_call(kernel, out_shape=[early] * 5 + [jax.ShapeDtypeStruct((5,...  82.3 us
    pallas_call x1, Pallas kernels, body(): pl.pallas_call(deliver, out_shape=[rows] * 5 + [sums], in_specs=[anywhere...  2.46 us

profile of v4, /device:TPU:1, one launch (start us, length us, event | category | flops | bytes accessed | tf_op | source)
XLA Modules:
  0.0 85.4 jit_solution(7155116672876521631)
XLA Ops:
  0.6 82.3 %hyena.1 = (bf16[128,3072]{1,0:T(8,128)(2,1)S(1)}, bf16[128,3072]{1,0:T(8,128)(2,1)S(1)}, bf16[128,3072]{1,0:T(8,128)(2,1)S(1)}, bf16[128,3072]{1,0:T(8,128)(2,1...) custom-call(bf16[128,4096]{1,0:T(8,128)(2,1)} %q_hbm.1, ...), custom_call_target="tpu_custom_call" | custom-call | tf_op jit(solution)/shard_map/hyena/pallas_call | solution.py:501
  82.9 2.5 %deliver.1 = (bf16[128,4096]{1,0:T(8,128)(2,1)}, bf16[128,4096]{1,0:T(8,128)(2,1)}, bf16[128,4096]{1,0:T(8,128)(2,1)}, bf16[128,4096]{1,0:T(8,128)(2,1)}, bf16[128,4096]{1,0:T(8,128)(2,1)}, /*index=5*/f32[32,128]{1,0:T(8,128)}) custom-call(bf16[128,3072]{1,0:T(8,128)(2,1)S(1)} %get-tuple-element.21.refs_0_, bf16[128,3072]{1,0:T(8,128)(2,1)S(1)} %get-tuple-element.22.refs_1_, ...), custom_call_target="tpu_custom_call" | custom-call | tf_op jit(solution)/shard_map/deliver/pallas_call | solution.py:553

commit v5 on v3

--- a/solution.py
+++ b/solution.py
@@ -78,6 +78,8 @@
     part,
     spec,
     sk_own,
+    sk_near,
+    sk_row,
     sk_all,
     load_sem,
     table_sem,
@@ -87,6 +89,8 @@
     out_recv,
     sk_send,
     sk_recv,
+    near_send,
+    near_recv,
 ):
     tokens, channels = q_hbm.shape
     width = channels // GROUPS
@@ -184,9 +188,25 @@
         ).start()
         lax.fori_loop(1, DEVICES, one, 0)
 
-    def send_out(g, place):
-        def one(k, carry):
-            o, i = target(k)
+    o_z = [lax.div(lax.rem(my_z + d, 4), 2) * 4 for d in range(4)]
+    i_z = [lax.rem(lax.rem(my_z + d, 4), 2) * 8 for d in range(4)]
+    o_y = [lax.rem(my_y + d, 4) for d in range(4)]
+    i_x = [lax.rem(my_x + d, 4) * 2 for d in range(4)]
+    i_c = [my_c, 1 - my_c]
+
+    def at_offset(c, x, y, z):
+        return o_z[z] + o_y[y], i_z[z] + i_x[x] + i_c[c]
+
+    offsets = [
+        (j % 2, j // 2 % 4, j // 8 % 4, j // 32)
+        for j in (k * ORDER % DEVICES for k in range(1, DEVICES))
+    ]
+
+    def hops(offset):
+        return sum(min(d, 4 - d) for d in offset[1:])
+
+    def send_out(g, place, far_first=False):
+        def to(o, i):
             pltpu.make_async_remote_copy(
                 src_ref=made.at[g, :, :, pl.ds((o * 16 + i) * 2, 2), :],
                 dst_ref=place.at[:, pl.ds(me * pairs, pairs)],
@@ -195,6 +215,9 @@
                 device_id=(o, i),
                 device_id_type=MESH,
             ).start()
+
+        def one(k, carry):
+            to(*target(k))
             return carry
 
         pltpu.make_async_copy(
@@ -202,7 +225,11 @@
             place.at[:, pl.ds(me * pairs, pairs)],
             out_recv.at[g],
         ).start()
-        lax.fori_loop(1, DEVICES, one, 0)
+        if far_first:
+            for offset in sorted(offsets, key=lambda f: hops(f) <= 2):
+                to(*at_offset(*offset))
+        else:
+            lax.fori_loop(1, DEVICES, one, 0)
 
     def transform(g, h):
         wr, wi = tw_ref[0], tw_ref[1]
@@ -262,32 +289,48 @@
         sk_own[...] = sk_own[...] + row
 
     def send_sums():
-        def one(k, carry):
-            pltpu.make_async_remote_copy(
-                src_ref=sk_own,
-                dst_ref=sk_all.at[pl.ds(me, 1), :],
-                send_sem=sk_send,
-                recv_sem=sk_recv,
-                device_id=target(k),
-                device_id_type=MESH,
-            ).start()
-            return carry
-
-        pltpu.make_async_copy(sk_own, sk_all.at[pl.ds(me, 1), :], sk_recv).start()
-        lax.fori_loop(1, DEVICES, one, 0)
+        own = sk_own[...]
+        sk_own[...] = jnp.where(my_c == 0, own, pltpu.roll(own, per * GROUPS, 1))
+        pltpu.make_async_remote_copy(
+            src_ref=sk_own,
+            dst_ref=sk_near,
+            send_sem=near_send,
+            recv_sem=near_recv,
+            device_id=at_offset(1, 0, 0, 0),
+            device_id_type=MESH,
+        ).start()
+        pltpu.make_async_copy(sk_near, sk_near, near_recv).wait()
+        sk_row[...] = sk_own[...] + sk_near[...]
+
+    def pass_sums():
+        chip = pl.ds(lax.div(me, 2), 1)
+        pltpu.make_async_copy(sk_row, sk_all.at[chip, :], sk_recv).start()
+        for offset in sorted(offsets, key=lambda f: hops(f) <= 2):
+            if offset[0] == 0:
+                pltpu.make_async_remote_copy(
+                    src_ref=sk_row,
+                    dst_ref=sk_all.at[chip, :],
+                    send_sem=sk_send,
+                    recv_sem=sk_recv,
+                    device_id=at_offset(*offset),
+                    device_id_type=MESH,
+                ).start()
 
     def spread_sums():
         pltpu.make_async_copy(sk_all, sk_all, sk_recv).wait()
-        rows = lax.broadcasted_iota(jnp.int32, (128, 128), 0)
-        cols = lax.broadcasted_iota(jnp.int32, (128, 128), 1)
-        mine = lax.div(cols, per) == lax.rem(rows, 16)
+        rows = lax.broadcasted_iota(jnp.int32, (64, 128), 0)
+        cols = lax.broadcasted_iota(jnp.int32, (64, 128), 1)
+        mine = lax.div(cols, 16) == lax.rem(rows, 8)
+        source = lax.broadcasted_iota(jnp.int32, (128, 128), 0)
+        place = lax.broadcasted_iota(jnp.int32, (128, 128), 1)
+        base = lax.rem(lax.div(place, per), 2) * (per * GROUPS) + lax.rem(place, per)
         for g in range(GROUPS):
-            pick = (rows == g * per + lax.rem(cols, per)).astype(F32)
+            pick = (source == base + g * per).astype(F32)
             wide = jnp.dot(
                 sk_all[...], pick, preferred_element_type=F32, precision=lax.Precision.HIGHEST
             )
             kept = jnp.where(mine, wide, 0.0)
-            sk_ref[g * 8 : g * 8 + 8, :] = jnp.sum(kept.reshape(8, 16, 128), axis=1) * (
+            sk_ref[g * 8 : g * 8 + 8, :] = jnp.sum(kept.reshape(8, 8, 128), axis=1) * (
                 1.0 / 128.0
             )
 
@@ -341,13 +384,17 @@
 
         lax.fori_loop(0, pairs // 2, half, 0)
 
+        @pl.when(g == GROUPS - 1)
+        def _():
+            pass_sums()
+
         @pl.when(g < GROUPS - 1)
         def _():
             send_out(g, back.at[g])
 
         @pl.when(g == GROUPS - 1)
         def _():
-            send_out(g, final)
+            send_out(g, final, far_first=True)
 
         return carry
 
@@ -361,7 +408,8 @@
     spread_sums()
     everyone = held.at[:, :, :, pl.ds(0, 2 * (DEVICES - 1)), :]
     pltpu.make_async_copy(everyone, everyone, in_send).wait()
-    sums = sk_all.at[pl.ds(0, DEVICES - 1), :]
+    pltpu.make_async_copy(sk_near, sk_near, near_send).wait()
+    sums = sk_all.at[pl.ds(0, DEVICES // 2 - 1), :]
     pltpu.make_async_copy(sums, sums, sk_send).wait()
     pltpu.make_async_copy(final, final, out_recv.at[GROUPS - 1]).wait()
     pltpu.make_async_copy(everyone, everyone, out_send).wait()
@@ -460,13 +508,17 @@
             pltpu.VMEM((3, 4, DEVICES, 256), BF),
             pltpu.VMEM((3, 4 * DEVICES, 256), BF),
             pltpu.VMEM((1, 128), F32),
-            pltpu.VMEM((DEVICES, 128), F32),
+            pltpu.VMEM((1, 128), F32),
+            pltpu.VMEM((1, 128), F32),
+            pltpu.VMEM((DEVICES // 2, 128), F32),
             dma((5, GROUPS)),
             dma((6,)),
             dma,
             dma((GROUPS,)),
             dma,
             dma((GROUPS,)),
+            dma,
+            dma,
             dma,
             dma,
         ],

time: 85.5 us -> 84.9 us (level)
  no operation moved by 1% of the time
where the time goes in v5:
time: 84.9 us; the launch traced here: 84.8 us
  Pallas kernels  84.1 us (99%)
    pallas_call x1, Pallas kernels, body(): pl.pallas_call(kernel, out_shape=[early] * 5 + [jax.ShapeDtypeStruct((5,...  81.7 us
    pallas_call x1, Pallas kernels, body(): pl.pallas_call(deliver, out_shape=[rows] * 5 + [sums], in_specs=[anywhere...  2.46 us

profile of v5, /device:TPU:1, one launch (start us, length us, event | category | flops | bytes accessed | tf_op | source)
XLA Modules:
  0.0 84.8 jit_solution(14729298297059139197)
XLA Ops:
  0.6 81.7 %hyena.1 = (bf16[128,3072]{1,0:T(8,128)(2,1)S(1)}, bf16[128,3072]{1,0:T(8,128)(2,1)S(1)}, bf16[128,3072]{1,0:T(8,128)(2,1)S(1)}, bf16[128,3072]{1,0:T(8,128)(2,1...) custom-call(bf16[128,4096]{1,0:T(8,128)(2,1)} %q_hbm.1, ...), custom_call_target="tpu_custom_call" | custom-call | tf_op jit(solution)/shard_map/hyena/pallas_call | solution.py:491
  82.3 2.5 %deliver.1 = (bf16[128,4096]{1,0:T(8,128)(2,1)}, bf16[128,4096]{1,0:T(8,128)(2,1)}, bf16[128,4096]{1,0:T(8,128)(2,1)}, bf16[128,4096]{1,0:T(8,128)(2,1)}, bf16[128,4096]{1,0:T(8,128)(2,1)}, /*index=5*/f32[32,128]{1,0:T(8,128)}) custom-call(bf16[128,3072]{1,0:T(8,128)(2,1)S(1)} %get-tuple-element.21.refs_0_, bf16[128,3072]{1,0:T(8,128)(2,1)S(1)} %get-tuple-element.22.refs_1_, ...), custom_call_target="tpu_custom_call" | custom-call | tf_op jit(solution)/shard_map/deliver/pallas_call | solution.py:543

commit v6 on v5

--- a/solution.py
+++ b/solution.py
@@ -15,6 +15,7 @@
 DEVICES = 128
 GROUPS = 4
 ORDER = 91
+REACH = 3
 VMEM_MAIN = 40
 VMEM_LAST = 16
 
@@ -91,6 +92,7 @@
     sk_recv,
     near_send,
     near_recv,
+    gate,
 ):
     tokens, channels = q_hbm.shape
     width = channels // GROUPS
@@ -112,18 +114,50 @@
         return lax.div(z, 2) * 4 + y, lax.rem(z, 2) * 8 + x * 2 + c
 
     barrier = pltpu.get_barrier_semaphore()
-    row = my_x * 2 + my_c
+    o_z = [lax.div(lax.rem(my_z + d, 4), 2) * 4 for d in range(4)]
+    i_z = [lax.rem(lax.rem(my_z + d, 4), 2) * 8 for d in range(4)]
+    o_y = [lax.rem(my_y + d, 4) for d in range(4)]
+    i_x = [lax.rem(my_x + d, 4) * 2 for d in range(4)]
+    i_c = [my_c, 1 - my_c]
+
+    def at_offset(c, x, y, z):
+        return o_z[z] + o_y[y], i_z[z] + i_x[x] + i_c[c]
+
+    offsets = [
+        (j % 2, j // 2 % 4, j // 8 % 4, j // 32)
+        for j in (k * ORDER % DEVICES for k in range(1, DEVICES))
+    ]
+
+    def hops(offset):
+        return sum(min(d, 4 - d) for d in offset[1:])
+
+    chips = sorted(
+        (f for f in offsets if f[0] == 0), key=lambda f: (hops(f) > REACH, -hops(f))
+    )
+    near_count = 2 * sum(hops(f) <= REACH for f in chips) + 1
+    far_count = 2 * sum(hops(f) > REACH for f in chips) + 1
+    partner = at_offset(1, 0, 0, 0)
 
     def greet():
-        for dz in (2, 1, 3, 0):
-            z = lax.rem(my_z + dz, 4)
-            base = lax.rem(z, 2) * 8
-            for dy in (2, 1, 3, 0):
-                o = lax.div(z, 2) * 4 + lax.rem(my_y + dy, 4)
-                alone = dz == 0 and dy == 0
-                for t in range(1 if alone else 0, 8):
-                    i = base + (lax.rem(row + t, 8) if alone else t)
-                    pl.semaphore_signal(barrier, inc=1, device_id=(o, i), device_id_type=MESH)
+        pl.semaphore_signal(barrier, inc=1, device_id=partner, device_id_type=MESH)
+        for _, x, y, z in chips:
+            core = 0 if hops((0, x, y, z)) <= REACH else 1
+            pl.semaphore_signal(
+                barrier,
+                inc=1,
+                device_id=(o_z[z] + o_y[y], i_z[z] + i_x[x] + core),
+                device_id_type=MESH,
+            )
+
+    def entered(core, count):
+        @pl.when(my_c == core)
+        def _():
+            pl.semaphore_wait(barrier, count)
+            pl.semaphore_signal(gate, inc=1, device_id=partner, device_id_type=MESH)
+
+        @pl.when(my_c != core)
+        def _():
+            pl.semaphore_wait(gate, 1)
 
     hbm_in = (k_hbm, v_hbm, g_hbm, q_hbm, h_hbm)
     K, V, G, Q, H = range(5)
@@ -168,9 +202,8 @@
 
         lax.fori_loop(0, width // 128, block, 0)
 
-    def send_in(g):
-        def one(k, carry):
-            o, i = target(k)
+    def send_in(g, first=False):
+        def to(o, i):
             pltpu.make_async_remote_copy(
                 src_ref=packed.at[g, :, pl.ds((o * 16 + i) * pairs, pairs)],
                 dst_ref=held.at[g, :, :, pl.ds(me * 2, 2), :],
@@ -179,6 +212,9 @@
                 device_id=(o, i),
                 device_id_type=MESH,
             ).start()
+
+        def one(k, carry):
+            to(*target(k))
             return carry
 
         pltpu.make_async_copy(
@@ -186,24 +222,17 @@
             held.at[g, :, :, pl.ds(me * 2, 2), :],
             in_recv.at[g],
         ).start()
-        lax.fori_loop(1, DEVICES, one, 0)
-
-    o_z = [lax.div(lax.rem(my_z + d, 4), 2) * 4 for d in range(4)]
-    i_z = [lax.rem(lax.rem(my_z + d, 4), 2) * 8 for d in range(4)]
-    o_y = [lax.rem(my_y + d, 4) for d in range(4)]
-    i_x = [lax.rem(my_x + d, 4) * 2 for d in range(4)]
-    i_c = [my_c, 1 - my_c]
-
-    def at_offset(c, x, y, z):
-        return o_z[z] + o_y[y], i_z[z] + i_x[x] + i_c[c]
-
-    offsets = [
-        (j % 2, j // 2 % 4, j // 8 % 4, j // 32)
-        for j in (k * ORDER % DEVICES for k in range(1, DEVICES))
-    ]
-
-    def hops(offset):
-        return sum(min(d, 4 - d) for d in offset[1:])
+        if first:
+            entered(0, near_count)
+            for offset in offsets:
+                if hops(offset) <= REACH:
+                    to(*at_offset(*offset))
+            entered(1, far_count)
+            for offset in offsets:
+                if hops(offset) > REACH:
+                    to(*at_offset(*offset))
+        else:
+            lax.fori_loop(1, DEVICES, one, 0)
 
     def send_out(g, place, far_first=False):
         def to(o, i):
@@ -296,7 +325,7 @@
             dst_ref=sk_near,
             send_sem=near_send,
             recv_sem=near_recv,
-            device_id=at_offset(1, 0, 0, 0),
+            device_id=partner,
             device_id_type=MESH,
         ).start()
         pltpu.make_async_copy(sk_near, sk_near, near_recv).wait()
@@ -356,8 +385,7 @@
 
     sk_own[...] = jnp.zeros_like(sk_own)
     prepare(0)
-    pl.semaphore_wait(barrier, DEVICES - 1)
-    send_in(0)
+    send_in(0, first=True)
 
     def ahead(g, carry):
         prepare(g)
@@ -521,6 +549,7 @@
             dma,
             dma,
             dma,
+            pltpu.SemaphoreType.REGULAR,
         ],
         compiler_params=pltpu.CompilerParams(
             collective_id=0, has_side_effects=True, vmem_limit_bytes=VMEM_MAIN * 1024 * 1024

time: 84.9 us -> 84.1 us (level)
  no operation moved by 1% of the time
where the time goes in v6:
time: 84.1 us; the launch traced here: 84 us
  Pallas kernels  83.3 us (99%)
    pallas_call x1, Pallas kernels, body(): pl.pallas_call(kernel, out_shape=[early] * 5 + [jax.ShapeDtypeStruct((5,...  80.9 us
    pallas_call x1, Pallas kernels, body(): pl.pallas_call(deliver, out_shape=[rows] * 5 + [sums], in_specs=[anywhere...  2.46 us

profile of v6, /device:TPU:1, one launch (start us, length us, event | category | flops | bytes accessed | tf_op | source)
XLA Modules:
  0.0 84.0 jit_solution(15002582201891487990)
XLA Ops:
  0.6 80.9 %hyena.1 = (bf16[128,3072]{1,0:T(8,128)(2,1)S(1)}, bf16[128,3072]{1,0:T(8,128)(2,1)S(1)}, bf16[128,3072]{1,0:T(8,128)(2,1)S(1)}, bf16[128,3072]{1,0:T(8,128)(2,1...) custom-call(bf16[128,4096]{1,0:T(8,128)(2,1)} %q_hbm.1, ...), custom_call_target="tpu_custom_call" | custom-call | tf_op jit(solution)/shard_map/hyena/pallas_call | solution.py:519
  81.5 2.5 %deliver.1 = (bf16[128,4096]{1,0:T(8,128)(2,1)}, bf16[128,4096]{1,0:T(8,128)(2,1)}, bf16[128,4096]{1,0:T(8,128)(2,1)}, bf16[128,4096]{1,0:T(8,128)(2,1)}, bf16[128,4096]{1,0:T(8,128)(2,1)}, /*index=5*/f32[32,128]{1,0:T(8,128)}) custom-call(bf16[128,3072]{1,0:T(8,128)(2,1)S(1)} %get-tuple-element.21.refs_0_, bf16[128,3072]{1,0:T(8,128)(2,1)S(1)} %get-tuple-element.22.refs_1_, ...), custom_call_target="tpu_custom_call" | custom-call | tf_op jit(solution)/shard_map/deliver/pallas_call | solution.py:572

commit v7 on v6

--- a/solution.py
+++ b/solution.py
@@ -15,7 +15,7 @@
 DEVICES = 128
 GROUPS = 4
 ORDER = 91
-REACH = 3
+REACH = 2
 VMEM_MAIN = 40
 VMEM_LAST = 16
 

time: 84.1 us -> 83.5 us (level)
  no operation moved by 1% of the time
where the time goes in v7:
time: 83.5 us; the launch traced here: 83.4 us
  Pallas kernels  82.8 us (99%)
    pallas_call x1, Pallas kernels, body(): pl.pallas_call(kernel, out_shape=[early] * 5 + [jax.ShapeDtypeStruct((5,...  80.3 us
    pallas_call x1, Pallas kernels, body(): pl.pallas_call(deliver, out_shape=[rows] * 5 + [sums], in_specs=[anywhere...  2.46 us

profile of v7, /device:TPU:1, one launch (start us, length us, event | category | flops | bytes accessed | tf_op | source)
XLA Modules:
  0.0 83.4 jit_solution(10732240429636835798)
XLA Ops:
  0.6 80.3 %hyena.1 = (bf16[128,3072]{1,0:T(8,128)(2,1)S(1)}, bf16[128,3072]{1,0:T(8,128)(2,1)S(1)}, bf16[128,3072]{1,0:T(8,128)(2,1)S(1)}, bf16[128,3072]{1,0:T(8,128)(2,1...) custom-call(bf16[128,4096]{1,0:T(8,128)(2,1)} %q_hbm.1, ...), custom_call_target="tpu_custom_call" | custom-call | tf_op jit(solution)/shard_map/hyena/pallas_call | solution.py:519
  80.9 2.5 %deliver.1 = (bf16[128,4096]{1,0:T(8,128)(2,1)}, bf16[128,4096]{1,0:T(8,128)(2,1)}, bf16[128,4096]{1,0:T(8,128)(2,1)}, bf16[128,4096]{1,0:T(8,128)(2,1)}, bf16[128,4096]{1,0:T(8,128)(2,1)}, /*index=5*/f32[32,128]{1,0:T(8,128)}) custom-call(bf16[128,3072]{1,0:T(8,128)(2,1)S(1)} %get-tuple-element.21.refs_0_, bf16[128,3072]{1,0:T(8,128)(2,1)S(1)} %get-tuple-element.22.refs_1_, ...), custom_call_target="tpu_custom_call" | custom-call | tf_op jit(solution)/shard_map/deliver/pallas_call | solution.py:572

commit v8 on v7

--- a/solution.py
+++ b/solution.py
@@ -224,11 +224,11 @@
         ).start()
         if first:
             entered(0, near_count)
-            for offset in offsets:
+            for offset in sorted(offsets, key=lambda f: -hops(f)):
                 if hops(offset) <= REACH:
                     to(*at_offset(*offset))
             entered(1, far_count)
-            for offset in offsets:
+            for offset in sorted(offsets, key=hops):
                 if hops(offset) > REACH:
                     to(*at_offset(*offset))
         else:

time: 83.5 us -> 83.5 us (level)
  no operation moved by 1% of the time
where the time goes in v8:
time: 83.5 us; the launch traced here: 83.4 us
  Pallas kernels  82.7 us (99%)
    pallas_call x1, Pallas kernels, body(): pl.pallas_call(kernel, out_shape=[early] * 5 + [jax.ShapeDtypeStruct((5,...  80.3 us
    pallas_call x1, Pallas kernels, body(): pl.pallas_call(deliver, out_shape=[rows] * 5 + [sums], in_specs=[anywhere...  2.46 us

profile of v8, /device:TPU:1, one launch (start us, length us, event | category | flops | bytes accessed | tf_op | source)
XLA Modules:
  0.0 83.4 jit_solution(3822254245931024424)
XLA Ops:
  0.6 80.3 %hyena.1 = (bf16[128,3072]{1,0:T(8,128)(2,1)S(1)}, bf16[128,3072]{1,0:T(8,128)(2,1)S(1)}, bf16[128,3072]{1,0:T(8,128)(2,1)S(1)}, bf16[128,3072]{1,0:T(8,128)(2,1...) custom-call(bf16[128,4096]{1,0:T(8,128)(2,1)} %q_hbm.1, ...), custom_call_target="tpu_custom_call" | custom-call | tf_op jit(solution)/shard_map/hyena/pallas_call | solution.py:519
  80.9 2.5 %deliver.1 = (bf16[128,4096]{1,0:T(8,128)(2,1)}, bf16[128,4096]{1,0:T(8,128)(2,1)}, bf16[128,4096]{1,0:T(8,128)(2,1)}, bf16[128,4096]{1,0:T(8,128)(2,1)}, bf16[128,4096]{1,0:T(8,128)(2,1)}, /*index=5*/f32[32,128]{1,0:T(8,128)}) custom-call(bf16[128,3072]{1,0:T(8,128)(2,1)S(1)} %get-tuple-element.21.refs_0_, bf16[128,3072]{1,0:T(8,128)(2,1)S(1)} %get-tuple-element.22.refs_1_, ...), custom_call_target="tpu_custom_call" | custom-call | tf_op jit(solution)/shard_map/deliver/pallas_call | solution.py:572
